TPU v7x, 16 devices: a 4x2x1 block of a 4x4x8 slice. The times are simulated.
16 devices in a mesh: dp: 2 (over y, z), tp: 8 (over x, core).
Axes of the slice: x: 4, y: 2, z: 1, core: 2. Of those that a mesh axis runs over, the one named last changes fastest.
The devices are a block of a 4x4x8 slice.
Arguments:
- token_ids: int32 [2, 1024], P('dp'), parts along dimension 0
- emb_table: bfloat16 [32000, 2048], P('tp')
- norm_gain: bfloat16 [2048], replicated
- grad_out: bfloat16 [2, 1024, 2048], P('dp', 'tp'), parts along dimension 0
Outputs:
- output 1: bfloat16 [2, 1024, 2048], P('dp', 'tp'), parts along dimension 0
- output 2: float32 [64000, 2048], P(('dp', 'tp')), parts along dimension 0
- output 3: float32 [4096], P('dp'), parts along dimension 0
There are 2 independent parts. A program takes and returns all parts, laid end to end along the dimension named above; an argument that names none is the same for every part.
All inputs are finite; a program needn't handle non-finite values.
Results may differ from a plain program's by a relative error of at most 0.0085353.
Values are sent between devices in bfloat16 or wider.
A program may use at most 768 MiB of HBM per device.

v0:
```python
import jax
import jax.numpy as jnp
from jax import lax
from jax.sharding import PartitionSpec as P

RMS_EPS = 1e-5


def norm_pass(embedded, norm_gain, grad_block):
    hidden_f32 = embedded.astype(jnp.float32)
    inv_rms = lax.rsqrt(jnp.mean(hidden_f32 * hidden_f32, axis=-1, keepdims=True) + RMS_EPS)
    x_hat = hidden_f32 * inv_rms
    normed = x_hat.astype(jnp.bfloat16) * norm_gain
    grad_f32 = grad_block.astype(jnp.float32)
    gain_part = jnp.sum(grad_f32 * x_hat, axis=(0, 1))
    grad_hat = grad_f32 * norm_gain.astype(jnp.float32)
    grad_in = (inv_rms * (grad_hat - x_hat * jnp.mean(grad_hat * x_hat, axis=-1, keepdims=True))).astype(jnp.bfloat16)
    return normed, grad_in, gain_part


def device_step(token_ids, table_block, norm_gain, grad_block):
    rows_block, hidden_size = table_block.shape
    tp_index = lax.axis_index('tp')
    local_ids = token_ids - tp_index * rows_block
    owned = (local_ids >= 0) & (local_ids < rows_block)
    looked_up = jnp.take(table_block, jnp.where(owned, local_ids, 0), axis=0)
    partial_rows = jnp.where(owned[:, :, None], looked_up, jnp.zeros((), jnp.bfloat16))
    embedded = lax.psum_scatter(partial_rows, 'tp', scatter_dimension=1, tiled=True)
    normed, grad_in, gain_part = norm_pass(embedded, norm_gain, grad_block)
    grad_gain = lax.psum(gain_part, 'tp')
    grad_all = lax.all_gather(grad_in, 'tp', axis=1, tiled=True)
    segment_ids = jnp.where(owned, local_ids, rows_block).reshape(-1)
    grad_table = jax.ops.segment_sum(grad_all.astype(jnp.float32).reshape(-1, hidden_size), segment_ids, num_segments=rows_block)
    return normed, grad_table, grad_gain


def solution(mesh):
    return jax.shard_map(device_step, mesh=mesh, in_specs=(P('dp', None), P('tp', None), P(None), P('dp', 'tp', None)), out_specs=(P('dp', 'tp', None), P(('dp', 'tp'), None), P('dp')), check_vma=False)
```

profile of v0, /device:TPU:113, one launch (start us, length us, event | category | flops | bytes accessed | tf_op | source)
XLA Modules:
  0.0 132.9 jit_solution(16394206325154145417)
XLA Ops:
  7.2 0.1 reduce-scatter.2.cloned.1.call-start
  7.2 0.7 and_reduce_fusion
  8.0 16.6 %gather_fusion = bf16[1024,2048]{1,0:T(8,128)(2,1)} fusion(bf16[4000,2048]{1,0:T(8,128)(2,1)} %param.5, s32[1024]{0:T(1024)S(1)} %broadcast_clamp_fusion), kind=kCustom, calls=%fused_computation | custom fusion | bytes 8392704 | tf_op jit(solution)/shard_map/jit(_take)/gather | solution.py:26
  24.6 4.1 %fusion.4 = bf16[1,1024,2048]{2,1,0:T(8,128)(2,1)} fusion(bf16[1024,2048]{1,0:T(8,128)(2,1)} %gather_fusion, pred[1024]{0:T(1024)(128)(4,1)S(1)} %get-tuple-element.5, pred[1024]{0:T(1024)(128)(4,1)S(1)} %get-tuple-element.7), kind=kLoop, calls=%fused_computation.7 | loop fusion | flops 4194304 | bytes 8390656 | tf_op jit(solution)/shard_map/jit(_where)/select_n | solution.py:27
  28.7 0.0 copy-start.1
  28.7 0.0 copy-start
  28.7 0.0 copy-start.2
  28.7 0.1 reduce-scatter.2.cloned.1.call-update
  28.7 0.1 all-gather.2.cloned.1.call-start
  28.8 0.5 copy-done.1
  29.4 33.4 %reduce-scatter.2.cloned.1.call-done = bf16[1,128,2048]{2,1,0:T(8,128)(2,1)} async-done(((bf16[1,1024,2048]{2,1,0:T(8,128)(2,1)}), bf16[1,128,2048]{2,1,0:T(8,128)(2,1)}) %reduce-scatter.2.cloned.1.call-update) | async-done | bytes 524304 | tf_op jit(solution)/shard_map/reduce_scatter | solution.py:28
  62.8 1.2 fusion.12
  64.0 0.0 copy-done
  64.0 1.5 %fusion.13 = (f32[2048]{0:T(1024)S(1)}, f32[128]{0:T(128)S(1)}) fusion(bf16[1,128,2048]{2,1,0:T(8,128)(2,1)} %reduce-scatter.2.cloned.1.call-done, bf16[1,128,2048]{2,1,0:T(8,128)(2,1)S(1)} %copy-done, f32[128]{0:T(128)S(1)} %add_rsqrt_fusion, f32[2048]{0:T(1024)S(1)} %convert_element_type.19), kind=kLoop, calls=%fused_computation.20 | loop fusion | flops 2094976 | bytes 1065984 | tf_op jit(solution)/shard_map/reduce_sum | solution.py:15
  65.5 2.2 %fusion.10 = bf16[1,128,2048]{2,1,0:T(8,128)(2,1)} fusion(bf16[1,128,2048]{2,1,0:T(8,128)(2,1)S(1)} %copy-done, bf16[1,128,2048]{2,1,0:T(8,128)(2,1)} %reduce-scatter.2.cloned.1.call-done, f32[128]{0:T(128)S(1)} %broadcast_multiply_fusion, f32[2048]{0:T(1024)S(1)} %convert_element_type.19, f32[128]{0:T(128)S(1)} %add_rsqrt_fusion), kind=kLoop, calls=%fused_computation.17 | loop fusion | flops 2097152 | bytes 1582080 | tf_op jit(solution)/shard_map/convert_element_type | solution.py:17
  67.7 0.1 all-gather.2.cloned.1.call-update
  67.8 0.0 copy-done.2
  67.8 17.1 %psum.7 = f32[2048]{0:T(1024)} all-reduce(f32[2048]{0:T(1024)S(1)} %get-tuple-element.3), channel_id=1, replica_groups=mesh['dp'=2,'tp'=8] {'tp'}, use_global_device_ids=true, to_apply=%region_5.6 | all-reduce | flops 2048 | bytes 16384 | tf_op jit(solution)/shard_map/psum | solution.py:30
  84.9 2.0 %fusion.14 = bf16[1,128,2048]{2,1,0:T(8,128)(2,1)} fusion(bf16[1,128,2048]{2,1,0:T(8,128)(2,1)} %reduce-scatter.2.cloned.1.call-done, f32[128]{0:T(128)S(1)} %add_rsqrt_fusion, bf16[2048]{0:T(1024)(128)(2,1)S(1)} %copy-done.1), kind=kLoop, calls=%fused_computation.21 | loop fusion | flops 1048576 | bytes 1053184 | tf_op jit(solution)/shard_map/mul | solution.py:13
  87.0 11.0 %all-gather.2.cloned.1.call-done = bf16[1,1024,2048]{2,1,0:T(8,128)(2,1)} async-done(((bf16[1,128,2048]{2,1,0:T(8,128)(2,1)}), bf16[1,1024,2048]{2,1,0:T(8,128)(2,1)}) %all-gather.2.cloned.1.call-update) | async-done | bytes 4194320 | tf_op jit(solution)/shard_map/all_gather | solution.py:31
  98.0 28.1 %scatter_custom_fusion = f32[4000,2048]{1,0:T(8,128)} fusion(s32[1024]{0:T(1024)S(1)} %bitcast.13, f32[]{:T(128)} %constant.15.clone.1, bf16[1,1024,2048]{2,1,0:T(8,128)(2,1)} %all-gather.2.cloned.1.call-done), kind=kCustom, calls=%fused_computation.2 | custom fusion | flops 4194304 | bytes 36962308 | tf_op jit(solution)/shard_map/scatter-add | solution.py:33
  (5 shorter events, 0.0 us)
Async XLA Ops:
  7.2 55.6 %reduce-scatter.2.cloned.1.call-start = ((), (), s32[]{:S(2)}) async-start(), calls=%async_computation.1 | async-start | bytes 4718592 | tf_op jit(solution)/shard_map/reduce_scatter | solution.py:28
  28.7 0.7 copy-start.1
  28.7 35.4 %copy-start = (bf16[1,128,2048]{2,1,0:T(8,128)(2,1)S(1)}, bf16[1,128,2048]{2,1,0:T(8,128)(2,1)}, u32[]{:S(2)}) copy-start(bf16[1,128,2048]{2,1,0:T(8,128)(2,1)} %param.7) | copy-start | bytes 1572868
  28.7 39.1 %copy-start.2 = (s32[1,1024]{1,0:T(1,128)S(1)}, s32[1,1024]{1,0:T(1,128)}, u32[]{:S(2)}) copy-start(s32[1,1024]{1,0:T(1,128)} %param.4) | copy-start | bytes 12292
  28.7 69.2 %all-gather.2.cloned.1.call-start = ((), (), s32[]{:S(2)}) async-start(), calls=%async_computation.2 | async-start | bytes 4718592 | tf_op jit(solution)/shard_map/all_gather | solution.py:31
Sparse Core Ops, SparseCore 0:
  28.9 33.9 reduce-scatter.1
  67.9 29.9 all-gather.1
where the time goes:
time: 133 us
  waiting for transfers between devices  44.5 us (33%)
  other arithmetic  39.9 us (30%)
  local copies, waits for them, and re-layouts  17.1 us (13%)
  blocking collectives  17.1 us (13%)
  between operations  14.1 us (11%)
    reduce_scatter x1, waiting for transfers between devices, device_step(): lax.psum_scatter(partial_rows, 'tp', scatter_dimension=1, tiled=True)  33.4 us
    scatter-add x1, other arithmetic, device_step(): jax.ops.segment_sum(grad_all.astype(jnp.float32).reshape(-1, hidden_size)...  28.1 us
    psum x1, blocking collectives, device_step(): grad_gain = lax.psum(gain_part, 'tp')  17.1 us
    gather x1, local copies, waits for them, and re-layouts, device_step(): looked_up = jnp.take(table_block, jnp.where(owned, local_ids, 0), axis=0)  16.6 us
    all_gather x1, waiting for transfers between devices, device_step(): grad_all = lax.all_gather(grad_in, 'tp', axis=1, tiled=True)  11 us
    select_n x1, other arithmetic, device_step(): jnp.where(owned[:, :, None], looked_up, jnp.zeros((), jnp.bfloat16))  4.1 us
  transfers between devices with their start and end apart: 2, of which 2 were waited for; matrix products, arithmetic and copies ran while one was open for 2% of the time, Pallas kernels for 0%

commit v1 on v0

v1 whole, which is shorter than its diff:
```python
import functools

import jax
import jax.numpy as jnp
from jax import lax
from jax.experimental import pallas as pl
from jax.experimental.pallas import tpu as pltpu
from jax.sharding import PartitionSpec as P

RMS_EPS = 1e-5
PAIR_ROWS = 40
MESH = pl.DeviceIdType.MESH
F32 = jnp.float32
BF16 = jnp.bfloat16


def exchange_kernel(n, x_out, dy_out, x_in, dy_in, dg_ref, dg_parts, x_send, x_recv, dy_send, dy_recv, dg_send, dg_recv):
    me = lax.axis_index('tp')
    dp = lax.axis_index('dp')
    hidden = x_out.shape[-1]
    barrier = pltpu.get_barrier_semaphore()
    for step in range(1, n):
        pl.semaphore_signal(barrier, inc=1, device_id=(dp, lax.rem(me + step, n)), device_id_type=MESH)
    pl.semaphore_wait(barrier, n - 1)

    def copies(src, dst, send_sem, recv_sem, step):
        peer = lax.rem(me + step, n)
        return pltpu.make_async_remote_copy(
            src_ref=src.at[peer], dst_ref=dst.at[me], send_sem=send_sem.at[step], recv_sem=recv_sem.at[step],
            device_id=(dp, peer), device_id_type=MESH)

    def arrival(dst, send_sem, recv_sem, step):
        source = lax.rem(me + n - step, n)
        return pltpu.make_async_remote_copy(
            src_ref=dst.at[source], dst_ref=dst.at[source], send_sem=send_sem.at[step], recv_sem=recv_sem.at[step],
            device_id=(dp, source), device_id_type=MESH)

    x_copies = [copies(x_out, x_in, x_send, x_recv, step) for step in range(1, n)]
    for copy in x_copies:
        copy.start()
    dy_copies = [copies(dy_out, dy_in, dy_send, dy_recv, step) for step in range(1, n)]
    for copy in dy_copies:
        copy.start()
    x_in[me] = x_out[me]
    dy_in[me] = dy_out[me]

    def dg_of(block):
        h = x_in[block].astype(F32)
        r = lax.rsqrt(jnp.mean(h * h, axis=-1, keepdims=True) + RMS_EPS)
        return jnp.sum(dy_out[block].astype(F32) * (h * r), axis=0, keepdims=True)

    part = dg_of(me)
    for step in range(1, n):
        arrival(x_in, x_send, x_recv, step).wait_recv()
        part = part + dg_of(lax.rem(me + n - step, n))
    dg_parts[me] = part

    def dg_copy(step):
        peer = lax.rem(me + step, n)
        return pltpu.make_async_remote_copy(
            src_ref=dg_parts.at[me], dst_ref=dg_parts.at[me], send_sem=dg_send.at[step], recv_sem=dg_recv.at[step],
            device_id=(dp, peer), device_id_type=MESH)

    dg_copies = [dg_copy(step) for step in range(1, n)]
    for copy in dg_copies:
        copy.start()
    for step in range(1, n):
        arrival(dy_in, dy_send, dy_recv, step).wait_recv()
    for step in range(1, n):
        arrival(dg_parts, dg_send, dg_recv, step).wait_recv()
    total = dg_parts[0]
    for i in range(1, n):
        total = total + dg_parts[i]
    dg_ref[...] = total
    for copy in x_copies + dy_copies + dg_copies:
        copy.wait_send()


def finish_kernel(zero_rows, target_ref, x_in, slot_ref, x_own, dy_in, g_ref, id_col, id_row, y_ref, de_ref, zeros, sums, zero_sem, row_sem):
    rows = de_ref.shape[0]
    slots = sums.shape[0]
    zeros[...] = jnp.zeros_like(zeros)
    zero_copies = [pltpu.make_async_copy(zeros, de_ref.at[pl.ds(i * zero_rows, zero_rows)], zero_sem.at[i]) for i in range(rows // zero_rows)]
    for copy in zero_copies:
        copy.start()
    gain = g_ref[...]
    gain32 = gain.astype(F32)

    def rms(h):
        return lax.rsqrt(jnp.mean(h * h, axis=-1, keepdims=True) + RMS_EPS)

    positions = y_ref.shape[0]
    pick = (slot_ref[...] == lax.broadcasted_iota(jnp.int32, (positions, slots), 1)).astype(BF16)
    h = jnp.dot(pick, x_in[...], preferred_element_type=F32)
    y_ref[...] = (h * rms(h)).astype(BF16) * gain

    h = x_own[...].astype(F32)
    r = rms(h)
    xh = h * r
    u = dy_in[...].astype(F32) * gain32
    dx = (r * (u - xh * jnp.mean(u * xh, axis=-1, keepdims=True))).astype(BF16)
    same = (id_col[...] == id_row[...]).astype(BF16)
    sums[...] = jnp.dot(same, dx, preferred_element_type=F32)
    for copy in zero_copies:
        copy.wait()

    def row_copy(k):
        return pltpu.make_async_copy(sums.at[pl.ds(k, 1)], de_ref.at[pl.ds(target_ref[k], 1)], row_sem)

    def start(k, _):
        @pl.when(target_ref[k] >= 0)
        def _():
            row_copy(k).start()
        return 0

    def wait(k, _):
        @pl.when(target_ref[k] >= 0)
        def _():
            row_copy(k).wait()
        return 0

    lax.fori_loop(0, slots, start, 0)
    lax.fori_loop(0, slots, wait, 0)


def divisor(rows, most):
    return max(d for d in range(8, most + 1, 8) if rows % d == 0)


def planned(n, cap, ids, table_block, norm_gain, grad_block):
    rows, hidden = table_block.shape
    positions = ids.shape[1]
    me = lax.axis_index('tp')
    before = (lax.broadcasted_iota(jnp.int32, (positions, positions), 0) < lax.broadcasted_iota(jnp.int32, (positions, positions), 1)).astype(jnp.int32)

    def slots_of(mask):
        return jnp.sum(mask.astype(jnp.int32)[:, :, None] * before[None], axis=1)

    local = ids - me * rows
    mine = (local >= 0) & (local < rows)
    slot = slots_of(mine)
    hit = mine[:, None, :] & (slot[:, None, :] == jnp.arange(cap)[None, :, None])
    wanted = jnp.sum(jnp.where(hit, local[:, None, :] + 1, 0), axis=-1).reshape(n * cap) - 1
    x_own = jnp.take(table_block, jnp.maximum(wanted, 0), axis=0)

    my_ids = lax.dynamic_index_in_dim(ids, me, 0, keepdims=True)
    starts = jnp.arange(n, dtype=jnp.int32)[:, None] * rows
    theirs = (my_ids >= starts) & (my_ids < starts + rows)
    their_slot = slots_of(theirs)
    hot = theirs[:, None, :] & (their_slot[:, None, :] == jnp.arange(cap)[None, :, None])
    dy_out = jnp.dot(hot.reshape(n * cap, positions).astype(BF16), grad_block.reshape(positions, hidden))
    slot_col = jnp.sum(jnp.where(theirs, jnp.arange(n)[:, None] * cap + their_slot, 0), axis=0)[:, None]

    earlier = (wanted[None, :] == wanted[:, None]) & (jnp.arange(n * cap)[None, :] < jnp.arange(n * cap)[:, None])
    target = jnp.where(jnp.any(earlier, axis=1), -1, wanted)

    slots_vmem = pltpu.VMEM((n, 1, hidden), F32)
    dma = pltpu.SemaphoreType.DMA((n,))
    x_in, dy_in, dg = pl.pallas_call(
        functools.partial(exchange_kernel, n),
        out_shape=(jax.ShapeDtypeStruct((n, cap, hidden), BF16), jax.ShapeDtypeStruct((n, cap, hidden), BF16), jax.ShapeDtypeStruct((1, hidden), F32)),
        in_specs=[pl.BlockSpec(memory_space=pltpu.VMEM)] * 2,
        out_specs=(pl.BlockSpec(memory_space=pltpu.VMEM),) * 3,
        scratch_shapes=[slots_vmem] + [dma] * 6,
        compiler_params=pltpu.CompilerParams(collective_id=cap, has_side_effects=True, vmem_limit_bytes=60 * 2**20),
        name=f'exchange{cap}',
    )(x_own.reshape(n, cap, hidden), dy_out.reshape(n, cap, hidden))

    zero_rows = divisor(rows, 256)
    y, grad_table = pl.pallas_call(
        functools.partial(finish_kernel, zero_rows),
        out_shape=(jax.ShapeDtypeStruct((positions, hidden), BF16), jax.ShapeDtypeStruct((rows, hidden), F32)),
        in_specs=[pl.BlockSpec(memory_space=pltpu.SMEM)] + [pl.BlockSpec(memory_space=pltpu.VMEM)] * 7,
        out_specs=(pl.BlockSpec(memory_space=pltpu.VMEM), pl.BlockSpec(memory_space=pl.ANY)),
        scratch_shapes=[pltpu.VMEM((zero_rows, hidden), F32), pltpu.VMEM((n * cap, hidden), F32), pltpu.SemaphoreType.DMA((rows // zero_rows,)), pltpu.SemaphoreType.DMA],
        compiler_params=pltpu.CompilerParams(vmem_limit_bytes=60 * 2**20),
        name=f'finish{cap}',
    )(target, x_in.reshape(n * cap, hidden), slot_col, x_own, dy_in.reshape(n * cap, hidden), norm_gain[None], wanted[:, None], wanted[None])
    return y.reshape(grad_block.shape), grad_table, dg.reshape(hidden)


def device_step(n, token_ids, table_block, norm_gain, grad_block):
    positions = grad_block.shape[0] * grad_block.shape[1]
    rows = table_block.shape[0]
    ids = token_ids.reshape(n, positions)
    owners = jnp.sum((ids[:, None, :] >= jnp.arange(1, n, dtype=jnp.int32)[None, :, None] * rows).astype(jnp.int32), axis=1)
    counts = jnp.sum((owners[:, None, :] == jnp.arange(n)[None, :, None]).astype(jnp.int32), axis=-1)
    cap = min(PAIR_ROWS, positions)
    args = (ids, table_block, norm_gain, grad_block)
    if cap == positions:
        return planned(n, cap, *args)
    return lax.cond(jnp.max(counts) <= cap, functools.partial(planned, n, cap), functools.partial(planned, n, positions), *args)


def solution(mesh):
    return jax.shard_map(functools.partial(device_step, mesh.shape['tp']), mesh=mesh, in_specs=(P('dp', None), P('tp', None), P(None), P('dp', 'tp', None)), out_specs=(P('dp', 'tp', None), P(('dp', 'tp'), None), P('dp')), check_vma=False)
```

time: 133 us -> 88.5 us (0.67)
  Pallas kernels: 0 us -> 59.8 us
  waiting for transfers between devices: 44.5 us -> 0 us
  other arithmetic: 39.9 us -> 7.11 us
  blocking collectives: 17.1 us -> 0 us
  between operations: 14.1 us -> 1.31 us
  matrix products: 0 us -> 2.62 us
    pallas_call x0 -> x2, Pallas kernels: none -> 59.8 us  [the longest x1 39.2 us: planned(): pl.pallas_call(functools.partial(exchange_kernel, n), out_shape=(jax.Shap...]
    reduce_scatter x1 -> x0, waiting for transfers between devices: 33.4 us -> none  [device_step(): lax.psum_scatter(partial_rows, 'tp', scatter_dimension=1, tiled=True)]
    scatter-add x1 -> x0, other arithmetic: 28.1 us -> none  [device_step(): jax.ops.segment_sum(grad_all.astype(jnp.float32).reshape(-1, hidden_size)...]
    psum x1 -> x0, blocking collectives: 17.1 us -> none  [device_step(): grad_gain = lax.psum(gain_part, 'tp')]
    all_gather x1 -> x0, waiting for transfers between devices: 11 us -> none  [device_step(): grad_all = lax.all_gather(grad_in, 'tp', axis=1, tiled=True)]
    gather x1, local copies, waits for them, and re-layouts: 16.6 us -> 12.1 us  [planned(): x_own = jnp.take(table_block, jnp.maximum(wanted, 0), axis=0)]
    dot_general x0 -> x1, matrix products: none -> 2.62 us  [planned(): jnp.dot(hot.reshape(n * cap, positions).astype(BF16), grad_block.reshape(...]
    broadcast_in_dim x0 -> x2, local copies, waits for them, and re-layouts: none -> 2.02 us  [the longest x1 1.29 us: planned(): norm_gain[None]]
  transfers between devices with their start and end apart: 2 -> 0, of which waited for: 2 -> 0; matrix products, arithmetic and copies ran while one was open for 2% -> 0% of each run, Pallas kernels for 0% -> 0%
where the time goes in v1:
time: 88.5 us; the launch traced here: 88.1 us
  Pallas kernels  59.8 us (68%)
  local copies, waits for them, and re-layouts  17 us (19%)
  other arithmetic  7.11 us (8%)
  matrix products  2.62 us (3%)
  between operations  1.31 us (1%)
    pallas_call x1, Pallas kernels, planned(): pl.pallas_call(functools.partial(exchange_kernel, n), out_shape=(jax.Shap...  39.2 us
    pallas_call x1, Pallas kernels, planned(): pl.pallas_call(functools.partial(finish_kernel, zero_rows), out_shape=(ja...  20.6 us
    gather x1, local copies, waits for them, and re-layouts, planned(): x_own = jnp.take(table_block, jnp.maximum(wanted, 0), axis=0)  12.1 us
    dot_general x1, matrix products, planned(): jnp.dot(hot.reshape(n * cap, positions).astype(BF16), grad_block.reshape(...  2.62 us
    select_n x2, other arithmetic, planned(): x_own = jnp.take(table_block, jnp.maximum(wanted, 0), axis=0)  2.51 us

profile of v1, /device:TPU:113, one launch (start us, length us, event | category | flops | bytes accessed | tf_op | source)
XLA Modules:
  0.0 88.1 jit_solution(17408035844266725812)
XLA Ops:
  0.6 0.8 convert_reduce_fusion.1
  1.4 0.2 convert_reduce_fusion
  1.6 0.6 reduce_max.9
  2.9 84.6 %conditional.1 = ((bf16[128,2048]{1,0:T(8,128)(2,1)}, f32[4000,2048]{1,0:T(8,128)}), f32[1,2048]{1,0:T(1,128)S(1)}) conditional(s32[]{:T(128)} %convert_element_type.51, (s32[8,128]{1,0:T(8,128)}, bf16[4000,2048]{1,0:T(8,128)(2,1)}, bf16[1,128,2048]{2,1,0:T(8,128)(2,1)}, bf16[2048]{0:T(1024)(128)(2,1)}) %tuple.34, (s32[8,128]{1,0:T(8,128)}, ...), branch_computations={%region_3.9_spmd, %region_9.15_spmd} | conditional | flops 546624384 | bytes 30173498 | solution.py:192
  3.2 0.7 dynamic-slice_bitcast_fusion.1
  3.9 0.1 fusion.26
  3.9 0.7 subtract_add_fusion.1
  4.6 0.7 fusion.25
  5.3 1.3 %broadcast_in_dim.86.g_ref = bf16[1,2048]{1,0:T(2,128)(2,1)} reshape(bf16[2048]{0:T(1024)(128)(2,1)} %get-tuple-element.30) | data formatting | bytes 8192 | tf_op jit(solution)/shard_map/cond/branch_1_fun/broadcast_in_dim | solution.py:178
  6.6 0.3 multiply_reduce_fusion.2
  7.0 0.2 select_reduce_fusion.2
  7.2 0.1 select_reduce_fusion.3
  7.3 0.1 sub.28
  7.4 0.6 sub.29.id_row
  8.0 0.1 sub.27
  8.1 0.2 fusion.15
  8.3 0.6 broadcast_select_fusion.5.target_ref
  8.9 0.7 copy.15.slot_ref
  9.7 0.8 copy.16.id_col
  10.5 2.6 %fusion.12.dy_out = bf16[8,40,2048]{2,1,0:T(8,128)(2,1)} fusion(bf16[1,128,2048]{2,1,0:T(8,128)(2,1)} %get-tuple-element.27, s32[8,128]{1,0:T(8,128)S(1)} %get-tuple-element.43, pred[8,128]{1,0:T(8,128)(4,1)S(1)} %get-tuple-element.52), kind=kOutput, calls=%fused_computation.38 | convolution fusion | flops 167854080 | bytes 1840128 | tf_op jit(solution)/shard_map/cond/branch_1_fun/dot_general | solution.py:151
  13.1 12.1 %gather_fusion.1 = bf16[320,2048]{1,0:T(8,128)(2,1)S(1)} fusion(bf16[4000,2048]{1,0:T(8,128)(2,1)} %get-tuple-element.26, s32[1024]{0:T(1024)S(1)} %pad_clamp_fusion), kind=kCustom, calls=%fused_computation.1 | custom fusion | bytes 2622720 | tf_op jit(solution)/shard_map/cond/branch_1_fun/jit(_take)/gather | solution.py:144
  25.2 1.2 %broadcast_select_fusion.4.x_out = bf16[8,40,2048]{2,1,0:T(8,128)(2,1)} fusion(bf16[8,40,2048]{2,1,0:T(8,128)(2,1)S(1)} %bitcast.37, pred[8,40]{1,0:T(8,128)(4,1)S(1)} %maximum_compare_fusion.2), kind=kLoop, calls=%fused_computation.37 | loop fusion | flops 655360 | bytes 2621760 | tf_op jit(solution)/shard_map/cond/branch_1_fun/jit(_take)/select_n | solution.py:144
  26.5 39.2 %exchange40.1 = (bf16[8,40,2048]{2,1,0:T(8,128)(2,1)}, bf16[8,40,2048]{2,1,0:T(8,128)(2,1)}, f32[1,2048]{1,0:T(1,128)S(1)}) custom-call(bf16[8,40,2048]{2,1,0:T(8,128)(2,1)} %broadcast_select_fusion.4.x_out, bf16[8,40,2048]{2,1,0:T(8,128)(2,1)} %fusion.12.dy_out), custom_call_target="tpu_custom_call" | custom-call | tf_op jit(solution)/shard_map/cond/branch_1_fun/exchange40/pallas_call | solution.py:159
  65.7 1.3 %broadcast_select_fusion.3.x_own = bf16[320,2048]{1,0:T(8,128)(2,1)} fusion(bf16[320,2048]{1,0:T(8,128)(2,1)S(1)} %gather_fusion.1, pred[320]{0:T(512)(128)(4,1)S(1)} %maximum_compare_fusion.3), kind=kLoop, calls=%fused_computation.36 | loop fusion | flops 655360 | bytes 2621760 | tf_op jit(solution)/shard_map/cond/branch_1_fun/jit(_take)/select_n | solution.py:144
  66.9 20.6 %finish40.1 = (bf16[128,2048]{1,0:T(8,128)(2,1)}, f32[4000,2048]{1,0:T(8,128)}) custom-call(s32[320]{0:T(512)} %broadcast_select_fusion.5.target_ref, bf16[320,2048]{1,0:T(8,128)(2,1)} %bitcast.40, s32[128,1]{1,0:T(8,128)} %copy.15.slot_ref, bf16[320,2048]{1,0:T(8,128)(2,1)} %broadcast_select_fusion.3.x_own, bf16[320,2048]{1,0:T(8,128)(2,1)} %bitcast.41, ...), custom_call_target="tpu_custom_call" | custom-call | tf_op jit(solution)/shard_map/cond/branch_1_fun/finish40/pallas_call | solution.py:170
  87.5 0.6 copy.24
  (9 shorter events, 0.1 us)

commit v2 on v1

v2 whole, which is shorter than its diff:
```python
import functools

import jax
import jax.numpy as jnp
from jax import lax
from jax.experimental import pallas as pl
from jax.experimental.pallas import tpu as pltpu
from jax.sharding import PartitionSpec as P

RMS_EPS = 1e-5
CORES = 2
X_ROWS = 40
DY_ROWS = 56
ZERO_FIRST = 12
MESH = pl.DeviceIdType.MESH
F32 = jnp.float32
BF16 = jnp.bfloat16
I32 = jnp.int32
NT = (((1,), (1,)), ((), ()))
TN = (((0,), (0,)), ((), ()))
LIMIT = 60 * 2**20


def iota(shape, dim):
    return lax.broadcasted_iota(I32, shape, dim)


def divisor(rows, most):
    return max(d for d in range(8, most + 1, 8) if rows % d == 0)


def rms(h):
    return lax.rsqrt(jnp.mean(h * h, axis=-1, keepdims=True) + RMS_EPS)


def column(row):
    size = row.shape[1]
    return jnp.sum(jnp.where(iota((size, size), 0) == iota((size, size), 1), row, 0.0), axis=1, keepdims=True)


def firsts(even, odd):
    size = even.shape[1]
    before = iota((size, size), 0) < iota((size, size), 1)
    even_col, odd_col = column(even), column(odd)
    even_dup = jnp.where((even_col == even) & before, 1.0, 0.0)
    odd_dup = jnp.where((even_col == odd) | ((odd_col == odd) & before), 1.0, 0.0)
    return 1.0 - jnp.max(even_dup, axis=0, keepdims=True), 1.0 - jnp.max(odd_dup, axis=0, keepdims=True)


def one_hots(mask, offset, cap):
    size = mask.shape[1]
    before = (iota((size, size), 0) < iota((size, size), 1)).astype(BF16)
    rank = jnp.dot(mask.astype(BF16), before, preferred_element_type=F32)
    if offset is not None:
        rank = rank + offset
    rank = jnp.where(mask > 0.0, rank, -1.0).astype(I32)
    slots = iota((cap, size), 0)
    return jnp.concatenate([jnp.where(rank[i:i + 1] == slots, 1.0, 0.0) for i in range(mask.shape[0])], axis=0)


def halves(ids):
    code = ids + 1
    return (code >> 8).astype(F32), (code & 255).astype(F32)


def unique_lists(even_mask, odd_mask, even_code, odd_code, cap):
    even_hot = one_hots(even_mask, None, cap)
    odd_hot = one_hots(odd_mask, jnp.sum(even_mask, axis=1, keepdims=True), cap)
    return (lax.dot_general(even_code.astype(BF16), even_hot.astype(BF16), NT, preferred_element_type=F32)
            + lax.dot_general(odd_code.astype(BF16), odd_hot.astype(BF16), NT, preferred_element_type=F32))


def within(ids, low, high):
    return jnp.where((ids >= low) & (ids < high), 1.0, 0.0)


def prepare_kernel(n, zero_rows, first, ids_ref, table_ref, de_ref, x_ref, list_ref, target_ref, flag_ref,
                   zeros, slabs, local, local_smem, targets, zero_sem, slab_sem, small_sem):
    me = lax.axis_index('tp')
    rows = de_ref.shape[0]
    chips = n // CORES
    slots = chips * X_ROWS
    zeros[...] = jnp.zeros_like(zeros)
    zero_copies = [pltpu.make_async_copy(zeros, de_ref.at[pl.ds(i * zero_rows, zero_rows)], zero_sem.at[i]) for i in range(first)]
    for copy in zero_copies:
        copy.start()

    ids = ids_ref[...]
    even = jnp.concatenate([ids[CORES * d:CORES * d + 1] for d in range(chips)], axis=0)
    odd = jnp.concatenate([ids[CORES * d + 1:CORES * d + 2] for d in range(chips)], axis=0)
    even_f, odd_f = even.astype(F32), odd.astype(F32)
    flags = [firsts(even_f[d:d + 1], odd_f[d:d + 1]) for d in range(chips)]
    even_first = jnp.concatenate([f[0] for f in flags], axis=0)
    odd_first = jnp.concatenate([f[1] for f in flags], axis=0)
    even_mine = within(even, me * rows, me * rows + rows) * even_first
    odd_mine = within(odd, me * rows, me * rows + rows) * odd_first
    even_code = jnp.concatenate(halves(even), axis=0)
    odd_code = jnp.concatenate(halves(odd), axis=0)
    product = unique_lists(even_mine, odd_mine, even_code, odd_code, X_ROWS)
    row_of, slot_of = iota(product.shape, 0), iota(product.shape, 1)
    own_block = (row_of % chips) == (slot_of // X_ROWS)
    wanted = jnp.sum(jnp.where(own_block, product * jnp.where(row_of < chips, 256.0, 1.0), 0.0), axis=0, keepdims=True) - 1.0
    row_in_block = jnp.maximum(wanted.astype(I32) - me * rows, 0)
    local[...] = jnp.broadcast_to(row_in_block, local.shape)
    to_smem = pltpu.make_async_copy(local, local_smem, small_sem.at[0])
    to_smem.start()
    to_smem.wait()

    def slab_copy(k):
        base = pl.multiple_of((local_smem[0, k] // 8) * 8, 8)
        return pltpu.make_async_copy(table_ref.at[pl.ds(base, 8)], slabs.at[k], slab_sem.at[k // X_ROWS])

    for d in range(chips):
        def start(s, _, d=d):
            slab_copy(d * X_ROWS + s).start()
            return 0
        lax.fori_loop(0, X_ROWS, start, 0)

    wanted_col = column(wanted)
    earlier = iota((slots, slots), 0) < iota((slots, slots), 1)
    repeated = jnp.max(jnp.where((wanted_col == wanted) & earlier, 1.0, 0.0), axis=0, keepdims=True)
    first_list = jnp.where(repeated > 0.0, -1.0, wanted)
    list_ref[...] = jnp.broadcast_to(first_list, list_ref.shape)
    targets[...] = jnp.broadcast_to(jnp.where(first_list >= 0.0, first_list - (me * rows).astype(F32), -1.0).astype(I32), targets.shape)
    out_targets = pltpu.make_async_copy(targets, target_ref, small_sem.at[1])
    out_targets.start()

    most = jnp.zeros((1, 1), F32)
    for i in range(n):
        held = within(even, i * rows, i * rows + rows) * even_first + within(odd, i * rows, i * rows + rows) * odd_first
        most = jnp.maximum(most, jnp.max(jnp.sum(held, axis=1, keepdims=True) * (1.0 / X_ROWS), axis=0, keepdims=True))
    for c in range(chips):
        held = jnp.sum(within(ids, c * CORES * rows, (c + 1) * CORES * rows), axis=1, keepdims=True)
        most = jnp.maximum(most, jnp.max(held * (1.0 / DY_ROWS), axis=0, keepdims=True))
    flag_ref[...] = jnp.broadcast_to(jnp.where(most > 1.0005, 0, 1), flag_ref.shape)

    remainder = column((row_in_block % 8).astype(F32)).astype(I32)
    hot_row, hot_col = iota((X_ROWS, X_ROWS * 8), 0), iota((X_ROWS, X_ROWS * 8), 1)
    for d in range(chips):
        def wait(s, _, d=d):
            pltpu.make_async_copy(table_ref.at[pl.ds(0, 8)], slabs.at[d * X_ROWS + s], slab_sem.at[d]).wait()
            return 0
        lax.fori_loop(0, X_ROWS, wait, 0)
        pick = jnp.where(hot_col == hot_row * 8 + remainder[d * X_ROWS:(d + 1) * X_ROWS], 1.0, 0.0).astype(BF16)
        block = slabs[pl.ds(d * X_ROWS, X_ROWS)].reshape(X_ROWS * 8, x_ref.shape[-1])
        x_ref[d] = jnp.dot(pick, block, preferred_element_type=F32).astype(BF16)
    out_targets.wait()
    for copy in zero_copies:
        copy.wait()


def exchange_kernel(n, rows, ids_ref, x_hbm, dy_hbm, xpos_ref, dy_all, dg_ref, x_own, dy_own, x_in, dy_out, dy_in, dg_parts,
                    local_sem, x_send, x_recv, xf_send, xf_recv, dy_send, dy_recv, dyf_send, dyf_recv, dg_send, dg_recv, out_sem):
    me = lax.axis_index('tp')
    dp = lax.axis_index('dp')
    chips = n // CORES
    chip = me // CORES
    core = me % CORES
    partner = chip * CORES + 1 - core
    barrier = pltpu.get_barrier_semaphore()
    for step in range(1, n):
        pl.semaphore_signal(barrier, inc=1, device_id=(dp, lax.rem(me + step, n)), device_id_type=MESH)
    load_dy = pltpu.make_async_copy(dy_hbm, dy_own, local_sem.at[0])
    load_dy.start()
    load_x = pltpu.make_async_copy(x_hbm, x_own, local_sem.at[1])
    load_x.start()

    my_ids = ids_ref[pl.ds(me, 1)]
    chip_masks = jnp.concatenate([within(my_ids, c * CORES * rows, (c + 1) * CORES * rows) for c in range(chips)], axis=0)
    dy_hot = one_hots(chip_masks, None, DY_ROWS).astype(BF16)
    load_dy.wait()
    for c in range(chips):
        dy_out[c] = jnp.dot(dy_hot[c * DY_ROWS:(c + 1) * DY_ROWS], dy_own[...], preferred_element_type=F32).astype(BF16)
    load_x.wait()
    pl.semaphore_wait(barrier, n - 1)

    def remote(src, dst, send_sem, recv_sem, device):
        return pltpu.make_async_remote_copy(src_ref=src, dst_ref=dst, send_sem=send_sem, recv_sem=recv_sem, device_id=(dp, device), device_id_type=MESH)

    sent = []

    def send_all(src, dst, send_sem, recv_sem, forward_send, forward_recv):
        for step in range(1, chips):
            there = lax.rem(chip + step, chips)
            copy = remote(src.at[there], dst.at[me], send_sem.at[step], recv_sem.at[step], there * CORES + core)
            copy.start()
            sent.append(copy)
        copy = remote(src.at[chip], dst.at[me], forward_send.at[0], forward_recv.at[0], partner)
        copy.start()
        sent.append(copy)
        dst[me] = src[chip]

    def source(step):
        return lax.rem(chip + chips - step, chips) * CORES

    def receive(dst, send_sem, recv_sem, forward_send, forward_recv, step):
        block = dst.at[source(step) + core]
        remote(block, block, send_sem.at[step], recv_sem.at[step], partner).wait_recv()
        copy = remote(block, block, forward_send.at[step], forward_recv.at[step], partner)
        copy.start()
        sent.append(copy)

    def receive_forwarded(dst, forward_send, forward_recv, step):
        block = dst.at[source(step) + 1 - core]
        remote(block, block, forward_send.at[step], forward_recv.at[step], partner).wait_recv()

    x_sems = (x_send, x_recv, xf_send, xf_recv)
    dy_sems = (dy_send, dy_recv, dyf_send, dyf_recv)
    send_all(x_own, x_in, *x_sems)
    send_all(dy_out, dy_in, *dy_sems)

    even, odd = ids_ref[pl.ds(chip * CORES, 1)], ids_ref[pl.ds(chip * CORES + 1, 1)]
    even_first, odd_first = firsts(even.astype(F32), odd.astype(F32))
    even_mask = jnp.concatenate([within(even, i * rows, (i + 1) * rows) for i in range(n)], axis=0) * even_first
    odd_mask = jnp.concatenate([within(odd, i * rows, (i + 1) * rows) for i in range(n)], axis=0) * odd_first
    pad = jnp.zeros((6, even.shape[1]), F32)
    even_code = jnp.concatenate(halves(even) + (pad,), axis=0)
    odd_code = jnp.concatenate(halves(odd) + (pad,), axis=0)
    product = unique_lists(even_mask, odd_mask, even_code, odd_code, X_ROWS)
    held = product[0:1] * 256.0 + product[1:2] - 1.0
    pick = jnp.where(column(my_ids.astype(F32)) == held, 1.0, 0.0).astype(BF16)

    order = [1, chips - 1] + list(range(2, chips - 1))
    for step in order:
        receive(x_in, *x_sems, step)
    for step in [0] + order:
        receive_forwarded(x_in, xf_send, xf_recv, step)
    hidden = xpos_ref.shape[-1]
    h = jnp.dot(pick, x_in[...].reshape(n * X_ROWS, hidden), preferred_element_type=F32)
    xpos_ref[...] = h.astype(BF16)
    dg_parts[me] = jnp.sum(dy_own[...].astype(F32) * (h * rms(h)), axis=0, keepdims=True)
    for step in range(1, n):
        copy = remote(dg_parts.at[me], dg_parts.at[me], dg_send.at[step], dg_recv.at[step], lax.rem(me + step, n))
        copy.start()
        sent.append(copy)

    outs = []

    def put(block):
        copy = pltpu.make_async_copy(dy_in.at[block], dy_all.at[block], out_sem.at[len(outs)])
        copy.start()
        outs.append(copy)

    put(me)
    for step in order:
        receive(dy_in, *dy_sems, step)
        put(source(step) + core)
    for step in [0] + order:
        receive_forwarded(dy_in, dyf_send, dyf_recv, step)
        put(source(step) + 1 - core)
    for step in range(1, n):
        block = dg_parts.at[lax.rem(me + n - step, n)]
        remote(block, block, dg_send.at[step], dg_recv.at[step], partner).wait_recv()
    total = dg_parts[0]
    for i in range(1, n):
        total = total + dg_parts[i]
    dg_ref[...] = total
    for copy in sent:
        copy.wait_send()
    for copy in outs:
        copy.wait()


def finish_kernel(n, zero_rows, first, target_ref, ids_ref, list_ref, xpos_ref, x_ref, dy_ref, g_ref, de_in, y_ref, de_ref,
                  zeros, dx_all, picks, sums, zero_sem, row_sem):
    me = lax.axis_index('tp')
    rows = de_ref.shape[0]
    slots = sums.shape[0]
    hidden = sums.shape[1]
    chip = me // CORES
    zeros[...] = jnp.zeros_like(zeros)
    zero_copies = [pltpu.make_async_copy(zeros, de_ref.at[pl.ds(i * zero_rows, zero_rows)], zero_sem.at[i]) for i in range(first, rows // zero_rows)]
    for copy in zero_copies:
        copy.start()
    gain = g_ref[...]
    gain32 = gain.astype(F32)
    h = xpos_ref[...].astype(F32)
    y_ref[...] = (h * rms(h)).astype(BF16) * gain

    ids = ids_ref[...]
    mask = within(ids, chip * CORES * rows, (chip + 1) * CORES * rows)
    hots = one_hots(mask, None, DY_ROWS)
    own_list = list_ref[0:1]
    x_own = x_ref[...].reshape(slots, hidden)
    for i in range(n):
        code = (ids[i:i + 1] + 2).astype(F32)
        row_ids = jnp.sum(hots[i * DY_ROWS:(i + 1) * DY_ROWS] * code, axis=1, keepdims=True) - 2.0
        picks[pl.ds(i * DY_ROWS, DY_ROWS)] = jnp.where(row_ids == own_list, 1.0, 0.0)

    def body(i, _):
        part = pl.ds(pl.multiple_of(i * DY_ROWS, DY_ROWS), DY_ROWS)
        h = jnp.dot(picks[part].astype(BF16), x_own, preferred_element_type=F32)
        r = rms(h)
        xh = h * r
        u = dy_ref[i].astype(F32) * gain32
        dx_all[part] = r * (u - xh * jnp.mean(u * xh, axis=-1, keepdims=True))
        return 0

    lax.fori_loop(0, n, body, 0)
    sums[...] = lax.dot_general(picks[...].astype(BF16), dx_all[...].astype(BF16), TN, preferred_element_type=F32)
    for copy in zero_copies:
        copy.wait()

    def row_copy(k):
        return pltpu.make_async_copy(sums.at[pl.ds(k, 1)], de_ref.at[pl.ds(target_ref[0, k], 1)], row_sem)

    def start(k, _):
        @pl.when(target_ref[0, k] >= 0)
        def _():
            row_copy(k).start()
        return 0

    def wait(k, _):
        @pl.when(target_ref[0, k] >= 0)
        def _():
            row_copy(k).wait()
        return 0

    lax.fori_loop(0, slots, start, 0)
    lax.fori_loop(0, slots, wait, 0)


def vmem():
    return pl.BlockSpec(memory_space=pltpu.VMEM)


def smem():
    return pl.BlockSpec(memory_space=pltpu.SMEM)


def anywhere():
    return pl.BlockSpec(memory_space=pl.ANY)


def dma(*shape):
    return pltpu.SemaphoreType.DMA(shape)


def fast_path(n, zero_rows, first, ids, grad_table, x_own, own_list, target, table_block, norm_gain, grad_block):
    rows, hidden = table_block.shape
    positions = ids.shape[1]
    chips = n // CORES
    slots = chips * X_ROWS
    xpos, dy_all, dg = pl.pallas_call(
        functools.partial(exchange_kernel, n, rows),
        out_shape=(jax.ShapeDtypeStruct((positions, hidden), BF16), jax.ShapeDtypeStruct((n, DY_ROWS, hidden), BF16), jax.ShapeDtypeStruct((1, hidden), F32)),
        in_specs=[vmem(), anywhere(), anywhere()],
        out_specs=(vmem(), anywhere(), vmem()),
        scratch_shapes=[
            pltpu.VMEM((chips, X_ROWS, hidden), BF16), pltpu.VMEM((positions, hidden), BF16),
            pltpu.VMEM((n, X_ROWS, hidden), BF16), pltpu.VMEM((chips, DY_ROWS, hidden), BF16), pltpu.VMEM((n, DY_ROWS, hidden), BF16),
            pltpu.VMEM((n, 1, hidden), F32), dma(2)] + [dma(chips)] * 8 + [dma(n)] * 3,
        compiler_params=pltpu.CompilerParams(collective_id=0, has_side_effects=True, vmem_limit_bytes=LIMIT),
        name='exchange_lists',
    )(ids, x_own, grad_block.reshape(positions, hidden))
    y, grad_table = pl.pallas_call(
        functools.partial(finish_kernel, n, zero_rows, first),
        out_shape=(jax.ShapeDtypeStruct((positions, hidden), BF16), jax.ShapeDtypeStruct((rows, hidden), F32)),
        in_specs=[smem()] + [vmem()] * 6 + [anywhere()],
        out_specs=(vmem(), anywhere()),
        input_output_aliases={7: 1},
        scratch_shapes=[
            pltpu.VMEM((zero_rows, hidden), F32), pltpu.VMEM((n * DY_ROWS, hidden), F32), pltpu.VMEM((n * DY_ROWS, slots), F32),
            pltpu.VMEM((slots, hidden), F32), dma(rows // zero_rows), pltpu.SemaphoreType.DMA],
        compiler_params=pltpu.CompilerParams(vmem_limit_bytes=LIMIT),
        name='finish_lists',
    )(target, ids, own_list, xpos, x_own, dy_all, norm_gain[None], grad_table)
    return y.reshape(grad_block.shape), grad_table, dg.reshape(hidden)


def pair_exchange_kernel(n, x_out, dy_out, x_in, dy_in, dg_ref, dg_parts, x_send, x_recv, dy_send, dy_recv, dg_send, dg_recv):
    me = lax.axis_index('tp')
    dp = lax.axis_index('dp')
    barrier = pltpu.get_barrier_semaphore()
    for step in range(1, n):
        pl.semaphore_signal(barrier, inc=1, device_id=(dp, lax.rem(me + step, n)), device_id_type=MESH)
    pl.semaphore_wait(barrier, n - 1)

    def copies(src, dst, send_sem, recv_sem, step):
        peer = lax.rem(me + step, n)
        return pltpu.make_async_remote_copy(
            src_ref=src.at[peer], dst_ref=dst.at[me], send_sem=send_sem.at[step], recv_sem=recv_sem.at[step],
            device_id=(dp, peer), device_id_type=MESH)

    def arrival(dst, send_sem, recv_sem, step):
        source = lax.rem(me + n - step, n)
        return pltpu.make_async_remote_copy(
            src_ref=dst.at[source], dst_ref=dst.at[source], send_sem=send_sem.at[step], recv_sem=recv_sem.at[step],
            device_id=(dp, source), device_id_type=MESH)

    x_copies = [copies(x_out, x_in, x_send, x_recv, step) for step in range(1, n)]
    for copy in x_copies:
        copy.start()
    dy_copies = [copies(dy_out, dy_in, dy_send, dy_recv, step) for step in range(1, n)]
    for copy in dy_copies:
        copy.start()
    x_in[me] = x_out[me]
    dy_in[me] = dy_out[me]

    def dg_of(block):
        h = x_in[block].astype(F32)
        return jnp.sum(dy_out[block].astype(F32) * (h * rms(h)), axis=0, keepdims=True)

    for step in range(1, n):
        arrival(x_in, x_send, x_recv, step).wait_recv()
    dg_parts[me] = lax.fori_loop(1, n, lambda i, total: total + dg_of(i), dg_of(0))

    def dg_copy(step):
        return pltpu.make_async_remote_copy(
            src_ref=dg_parts.at[me], dst_ref=dg_parts.at[me], send_sem=dg_send.at[step], recv_sem=dg_recv.at[step],
            device_id=(dp, lax.rem(me + step, n)), device_id_type=MESH)

    dg_copies = [dg_copy(step) for step in range(1, n)]
    for copy in dg_copies:
        copy.start()
    for step in range(1, n):
        arrival(dy_in, dy_send, dy_recv, step).wait_recv()
    for step in range(1, n):
        arrival(dg_parts, dg_send, dg_recv, step).wait_recv()
    total = dg_parts[0]
    for i in range(1, n):
        total = total + dg_parts[i]
    dg_ref[...] = total
    for copy in x_copies + dy_copies + dg_copies:
        copy.wait_send()


def any_path(n, ids, table_block, norm_gain, grad_block):
    rows, hidden = table_block.shape
    positions = ids.shape[1]
    cap = positions
    me = lax.axis_index('tp')
    before = (iota((positions, positions), 0) < iota((positions, positions), 1)).astype(I32)

    def slots_of(mask):
        return jnp.sum(mask.astype(I32)[:, :, None] * before[None], axis=1)

    local = ids - me * rows
    mine = (local >= 0) & (local < rows)
    slot = slots_of(mine)
    hit = mine[:, None, :] & (slot[:, None, :] == jnp.arange(cap)[None, :, None])
    wanted = jnp.sum(jnp.where(hit, local[:, None, :] + 1, 0), axis=-1).reshape(n * cap) - 1
    x_own = jnp.take(table_block, jnp.maximum(wanted, 0), axis=0)
    my_ids = lax.dynamic_index_in_dim(ids, me, 0, keepdims=True)
    starts = jnp.arange(n, dtype=I32)[:, None] * rows
    theirs = (my_ids >= starts) & (my_ids < starts + rows)
    their_slot = slots_of(theirs)
    hot = theirs[:, None, :] & (their_slot[:, None, :] == jnp.arange(cap)[None, :, None])
    dy_out = jnp.dot(hot.reshape(n * cap, positions).astype(BF16), grad_block.reshape(positions, hidden))
    slot_of = jnp.sum(jnp.where(theirs, jnp.arange(n)[:, None] * cap + their_slot, 0), axis=0)
    x_in, dy_in, dg = pl.pallas_call(
        functools.partial(pair_exchange_kernel, n),
        out_shape=(jax.ShapeDtypeStruct((n, cap, hidden), BF16), jax.ShapeDtypeStruct((n, cap, hidden), BF16), jax.ShapeDtypeStruct((1, hidden), F32)),
        in_specs=[vmem(), vmem()],
        out_specs=(vmem(), vmem(), vmem()),
        scratch_shapes=[pltpu.VMEM((n, 1, hidden), F32)] + [dma(n)] * 6,
        compiler_params=pltpu.CompilerParams(collective_id=1, has_side_effects=True, vmem_limit_bytes=LIMIT),
        name='exchange_pairs',
    )(x_own.reshape(n, cap, hidden), dy_out.reshape(n, cap, hidden))
    h = jnp.take(x_in.reshape(n * cap, hidden), slot_of, axis=0).astype(F32)
    y = (h * rms(h)).astype(BF16) * norm_gain
    h = x_own.astype(F32)
    r = rms(h)
    xh = h * r
    u = dy_in.reshape(n * cap, hidden).astype(F32) * norm_gain.astype(F32)
    dx = (r * (u - xh * jnp.mean(u * xh, axis=-1, keepdims=True))).astype(BF16)
    grad_table = jax.ops.segment_sum(dx.astype(F32), jnp.where(wanted >= 0, wanted, rows), num_segments=rows)
    return y.reshape(grad_block.shape), grad_table, dg.reshape(hidden)


def device_step(n, token_ids, table_block, norm_gain, grad_block):
    positions = grad_block.shape[0] * grad_block.shape[1]
    rows, hidden = table_block.shape
    ids = token_ids.reshape(n, positions)
    chips = n // CORES
    slots = chips * X_ROWS
    zero_rows = divisor(rows, 256)
    first = min(ZERO_FIRST, rows // zero_rows)
    grad_table, x_own, own_list, target, flag = pl.pallas_call(
        functools.partial(prepare_kernel, n, zero_rows, first),
        out_shape=(jax.ShapeDtypeStruct((rows, hidden), F32), jax.ShapeDtypeStruct((chips, X_ROWS, hidden), BF16),
                   jax.ShapeDtypeStruct((8, slots), F32), jax.ShapeDtypeStruct((8, slots), I32), jax.ShapeDtypeStruct((8, 128), I32)),
        in_specs=[vmem(), anywhere()],
        out_specs=(anywhere(), vmem(), vmem(), anywhere(), vmem()),
        scratch_shapes=[
            pltpu.VMEM((zero_rows, hidden), F32), pltpu.VMEM((slots, 8, hidden), BF16), pltpu.VMEM((8, slots), I32), pltpu.SMEM((8, slots), I32),
            pltpu.VMEM((8, slots), I32), dma(first), dma(chips), dma(2)],
        compiler_params=pltpu.CompilerParams(vmem_limit_bytes=LIMIT),
        name='prepare',
    )(ids, table_block)

    def fast(ids, grad_table, x_own, own_list, target, *rest):
        return fast_path(n, zero_rows, first, ids, grad_table, x_own, own_list, target, *rest)

    def slow(ids, grad_table, x_own, own_list, target, *rest):
        return any_path(n, ids, *rest)

    return lax.cond(flag[0, 0] > 0, fast, slow, ids, grad_table, x_own, own_list, target, table_block, norm_gain, grad_block)


def solution(mesh):
    return jax.shard_map(functools.partial(device_step, mesh.shape['tp']), mesh=mesh, in_specs=(P('dp', None), P('tp', None), P(None), P('dp', 'tp', None)), out_specs=(P('dp', 'tp', None), P(('dp', 'tp'), None), P('dp')), check_vma=False)
```

time: 88.5 us -> 52.8 us (0.60)
  local copies, waits for them, and re-layouts: 17 us -> 2.42 us
  Pallas kernels: 59.8 us -> 48.3 us
  other arithmetic: 7.11 us -> 0 us
  matrix products: 2.62 us -> 0 us
    gather x1 -> x0, local copies, waits for them, and re-layouts: 12.1 us -> none  [planned(): x_own = jnp.take(table_block, jnp.maximum(wanted, 0), axis=0)]
    pallas_call x2 -> x3, Pallas kernels: 59.8 us -> 48.3 us  [the longest x1 27.4 us: fast_path(): pl.pallas_call(functools.partial(exchange_kernel, n, rows), out_shape=(ja...]
    select_n x3 -> x0, other arithmetic: 3.1 us -> none  [the longest x2 2.51 us: planned(): x_own = jnp.take(table_block, jnp.maximum(wanted, 0), axis=0)]
    dot_general x1 -> x0, matrix products: 2.62 us -> none  [planned(): jnp.dot(hot.reshape(n * cap, positions).astype(BF16), grad_block.reshape(...]
    reduce_sum x5 -> x0, other arithmetic: 1.61 us -> none  [the longest x1 0.76 us: device_step(): jnp.sum((ids[:, None, :] >= jnp.arange(1, n, dtype=jnp.int32)[None, :, No...]
    sub x4 -> x0, local copies, waits for them, and re-layouts: 1.58 us -> none  [planned(): jnp.sum(jnp.where(hit, local[:, None, :] + 1, 0), axis=-1).reshape(n * cap)]
    broadcast_in_dim x2 -> x1, local copies, waits for them, and re-layouts: 2.02 us -> 0.6 us  [fast_path(): norm_gain[None]]
    slice x0 -> x1, local copies, waits for them, and re-layouts: none -> 1.2 us  [device_step(): flag[0, 0] > 0]
where the time goes in v2:
time: 52.8 us; the launch traced here: 52.4 us
  Pallas kernels  48.3 us (91%)
  local copies, waits for them, and re-layouts  2.42 us (5%)
  between operations  1.35 us (3%)
    pallas_call x1, Pallas kernels, fast_path(): pl.pallas_call(functools.partial(exchange_kernel, n, rows), out_shape=(ja...  27.4 us
    pallas_call x1, Pallas kernels, fast_path(): pl.pallas_call(functools.partial(finish_kernel, n, zero_rows, first), out...  11.3 us
    pallas_call x1, Pallas kernels, device_step(): pl.pallas_call(functools.partial(prepare_kernel, n, zero_rows, first), ou...  9.66 us
    slice x1, local copies, waits for them, and re-layouts, device_step(): flag[0, 0] > 0  1.2 us

profile of v2, /device:TPU:113, one launch (start us, length us, event | category | flops | bytes accessed | tf_op | source)
XLA Modules:
  0.0 52.4 jit_solution(11352015743994880461)
XLA Ops:
  0.6 0.0 copy-start.2
  0.6 0.0 copy-start.4
  0.7 0.0 copy-start.3
  0.7 9.7 %prepare.1 = (f32[4000,2048]{1,0:T(8,128)}, bf16[4,40,2048]{2,1,0:T(8,128)(2,1)S(1)}, f32[8,160]{1,0:T(8,128)S(1)}, s32[8,160]{1,0:T(8,128)S(1)}, s32[8,128]{1,0:T(8,128)}) custom-call(s32[8,128]{1,0:T(8,128)} %bitcast.43, bf16[4000,2048]{1,0:T(8,128)(2,1)} %table_ref.1), custom_call_target="tpu_custom_call" | custom-call | tf_op jit(solution)/shard_map/prepare/pallas_call | solution.py:479
  10.3 1.2 %slice.3 = s32[1,1]{1,0:T(1,128)} slice(s32[8,128]{1,0:T(8,128)} %get-tuple-element.49), slice={[0:1], [0:1]} | slice | bytes 8 | tf_op jit(solution)/shard_map/slice | solution.py:498
  12.2 0.0 copy-done.2
  12.2 0.0 copy-done.4
  12.2 0.0 copy-done.3
  12.2 39.5 %conditional.1 = (bf16[1,128,2048]{2,1,0:T(8,128)(2,1)}, f32[4000,2048]{1,0:T(8,128)}, f32[2048]{0:T(1024)S(1)}) conditional(s32[]{:T(128)} %bitcast.21, (s32[8,128]{1,0:T(8,128)S(1)}, bf16[4000,2048]{1,0:T(8,128)(2,1)}, bf16[1,128,2048]{2,1,0:T(8,128)(2,1)S(1)}, bf16[2048]{0:T(1024)(128)(2,1)S(1)}) %tuple.37, (bf16[1,128,2048]{2,1,0:T(8,128)(2,1)S(1)}, ...), branch_computations={%region_0.9_spmd, %region_9.10_spmd} | conditional | flops 588835968 | bytes 120125672 | solution.py:498
  12.5 0.6 %broadcast_in_dim.67.g_ref = bf16[1,2048]{1,0:T(2,128)(2,1)} reshape(bf16[2048]{0:T(1024)(128)(2,1)S(1)} %get-tuple-element.36) | data formatting | bytes 8192 | tf_op jit(solution)/shard_map/cond/branch_1_fun/broadcast_in_dim | solution.py:367
  13.1 27.4 %exchange_lists.1 = (bf16[128,2048]{1,0:T(8,128)(2,1)}, bf16[8,56,2048]{2,1,0:T(8,128)(2,1)}, f32[1,2048]{1,0:T(1,128)S(1)}) custom-call(s32[8,128]{1,0:T(8,128)S(1)} %get-tuple-element.30.ids_ref, bf16[4,40,2048]{2,1,0:T(8,128)(2,1)S(1)} %get-tuple-element.32.x_hbm.x_ref, bf16[128,2048]{1,0:T(8,128)(2,1)S(1)} %bitcast.41), custom_call_target="tpu_custom_call" | custom-call | tf_op jit(solution)/shard_map/cond/branch_1_fun/exchange_lists/pallas_call | solution.py:344
  40.4 11.3 %finish_lists.1 = (bf16[128,2048]{1,0:T(8,128)(2,1)}, f32[4000,2048]{1,0:T(8,128)}) custom-call(s32[8,160]{1,0:T(8,128)S(1)} %get-tuple-element.29.target_ref, s32[8,128]{1,0:T(8,128)S(1)} %get-tuple-element.30.ids_ref, f32[8,160]{1,0:T(8,128)S(1)} %get-tuple-element.31.list_ref, ...), custom_call_target="tpu_custom_call", output_to_operand_aliasing={{1}: (7, {})} | custom-call | tf_op jit(solution)/shard_map/cond/branch_1_fun/finish_lists/pallas_call | solution.py:356
  51.8 0.6 %copy.22 = f32[2048]{0:T(1024)} copy(f32[2048]{0:T(1024)S(1)} %get-tuple-element.80) | data formatting | bytes 16384
Async XLA Ops:
  0.6 11.6 %copy-start.2 = (bf16[1,128,2048]{2,1,0:T(8,128)(2,1)S(1)}, bf16[1,128,2048]{2,1,0:T(8,128)(2,1)}, u32[]{:S(2)}) copy-start(bf16[1,128,2048]{2,1,0:T(8,128)(2,1)} %param.9) | copy-start | bytes 1572868
  0.6 11.6 %copy-start.4 = (bf16[2048]{0:T(1024)(128)(2,1)S(1)}, bf16[2048]{0:T(1024)(128)(2,1)}, u32[]{:S(2)}) copy-start(bf16[2048]{0:T(1024)(128)(2,1)} %param.8) | copy-start | bytes 12292
  0.7 11.6 %copy-start.3 = (s32[1,1024]{1,0:T(1,128)S(1)}, s32[1,1024]{1,0:T(1,128)}, u32[]{:S(2)}) copy-start(s32[1,1024]{1,0:T(1,128)} %param.6) | copy-start | bytes 12292

commit v3 on v0

v3 whole, which is shorter than its diff:
```python
import functools

import jax
import jax.numpy as jnp
from jax import lax
from jax.experimental import pallas as pl
from jax.experimental.pallas import tpu as pltpu
from jax.sharding import PartitionSpec as P

RMS_EPS = 1e-5
CORES = 2
X_ROWS = 40
DY_ROWS = 56
ZERO_ROWS = 80
MESH = pl.DeviceIdType.MESH
F32 = jnp.float32
BF16 = jnp.bfloat16
I32 = jnp.int32
NT = (((1,), (1,)), ((), ()))
TN = (((0,), (0,)), ((), ()))
LIMIT = 60 * 2**20


def iota(shape, dim):
    return lax.broadcasted_iota(I32, shape, dim)


def divisor(rows, most):
    return max(d for d in range(8, most + 1, 8) if rows % d == 0)


def rms(h):
    return lax.rsqrt(jnp.mean(h * h, axis=-1, keepdims=True) + RMS_EPS)


def column(row):
    size = row.shape[1]
    return jnp.sum(jnp.where(iota((size, size), 0) == iota((size, size), 1), row, 0.0), axis=1, keepdims=True)


def firsts(even, odd):
    size = even.shape[1]
    before = iota((size, size), 0) < iota((size, size), 1)
    even_col, odd_col = column(even), column(odd)
    even_dup = jnp.where((even_col == even) & before, 1.0, 0.0)
    odd_dup = jnp.where((even_col == odd) | ((odd_col == odd) & before), 1.0, 0.0)
    return 1.0 - jnp.max(even_dup, axis=0, keepdims=True), 1.0 - jnp.max(odd_dup, axis=0, keepdims=True)


def one_hots(mask, offset, cap):
    size = mask.shape[1]
    before = (iota((size, size), 0) < iota((size, size), 1)).astype(BF16)
    rank = jnp.dot(mask.astype(BF16), before, preferred_element_type=F32)
    if offset is not None:
        rank = rank + offset
    rank = jnp.where(mask > 0.0, rank, -1.0).astype(I32)
    slots = iota((cap, size), 0)
    return jnp.concatenate([jnp.where(rank[i:i + 1] == slots, 1.0, 0.0) for i in range(mask.shape[0])], axis=0)


def halves(ids):
    code = ids + 1
    return (code >> 8).astype(F32), (code & 255).astype(F32)


def unique_lists(even_mask, odd_mask, even_code, odd_code, cap):
    even_hot = one_hots(even_mask, None, cap)
    odd_hot = one_hots(odd_mask, jnp.sum(even_mask, axis=1, keepdims=True), cap)
    return (lax.dot_general(even_code.astype(BF16), even_hot.astype(BF16), NT, preferred_element_type=F32)
            + lax.dot_general(odd_code.astype(BF16), odd_hot.astype(BF16), NT, preferred_element_type=F32))


def wide(lines):
    lines = lines.astype(F32)
    return jnp.concatenate([lines[i:i + 1] for i in range(lines.shape[0])], axis=1)


def within(ids, low, high):
    return jnp.where((ids >= low) & (ids < high), 1.0, 0.0)


def exchange_kernel(n, rows, ids_ref, table_hbm, dy_own, g_ref, xpos_ref, sums_ref, dg_ref, target_ref, over_ref,
                    table, slabs, local, local_smem, x_own, x_in, dy_out, dy_in, picks, spots, dx_all, dg_parts,
                    table_sem, small_sem, x_send, x_recv, xf_send, xf_recv, dy_send, dy_recv, dyf_send, dyf_recv, dg_send, dg_recv):
    chips = n // CORES
    me = lax.axis_index('tp')
    dp = lax.axis_index('dp')
    chip = me // CORES
    core = me % CORES
    partner = chip * CORES + 1 - core
    slots, hidden = sums_ref.shape
    barrier = pltpu.get_barrier_semaphore()
    for step in range(1, n):
        pl.semaphore_signal(barrier, inc=1, device_id=(dp, lax.rem(me + step, n)), device_id_type=MESH)
    pieces = table_sem.shape[0]
    piece = table_hbm.shape[0] // pieces
    table_copies = [pltpu.make_async_copy(table_hbm.at[pl.ds(i * piece, piece)], table.at[pl.ds(i * piece, piece)], table_sem.at[i]) for i in range(pieces)]
    for copy in table_copies:
        copy.start()

    def remote(src, dst, send_sem, recv_sem, device):
        return pltpu.make_async_remote_copy(src_ref=src, dst_ref=dst, send_sem=send_sem, recv_sem=recv_sem, device_id=(dp, device), device_id_type=MESH)

    sent = []

    def send(*args):
        copy = remote(*args)
        copy.start()
        sent.append(copy)

    def source(step):
        return lax.rem(chip + chips - step, chips)

    def device_at(step):
        return lax.rem(chip + step, chips) * CORES + core

    order = [1, chips - 1] + list(range(2, chips - 1))
    low = me * rows

    my_ids = ids_ref[pl.ds(me, 1)]
    near = [lax.rem(chip + step, chips) for step in range(chips)]
    masks = jnp.concatenate([within(my_ids, c * CORES * rows, (c + 1) * CORES * rows) for c in near], axis=0)
    hots = one_hots(masks, None, DY_ROWS).astype(BF16)
    for step in range(chips):
        dy_out[step] = jnp.dot(hots[step * DY_ROWS:(step + 1) * DY_ROWS], dy_own[...], preferred_element_type=F32).astype(BF16)
    pl.semaphore_wait(barrier, n - 1)
    for step in order:
        send(dy_out.at[step], dy_in.at[me], dy_send.at[step], dy_recv.at[step], device_at(step))
    send(dy_out.at[0], dy_in.at[me], dyf_send.at[0], dyf_recv.at[0], partner)
    dy_in[me] = dy_out[0]

    even = jnp.concatenate([ids_ref[pl.ds(c * CORES, 1)] for c in near], axis=0)
    odd = jnp.concatenate([ids_ref[pl.ds(c * CORES + 1, 1)] for c in near], axis=0)
    near_even, near_odd = even, odd
    even_f, odd_f = even.astype(F32), odd.astype(F32)
    flags = [firsts(even_f[d:d + 1], odd_f[d:d + 1]) for d in range(chips)]
    even_first = jnp.concatenate([f[0] for f in flags], axis=0)
    odd_first = jnp.concatenate([f[1] for f in flags], axis=0)
    even_code = jnp.concatenate(halves(even), axis=0)
    odd_code = jnp.concatenate(halves(odd), axis=0)
    product = unique_lists(within(even, low, low + rows) * even_first, within(odd, low, low + rows) * odd_first, even_code, odd_code, X_ROWS)
    row_of, slot_of = iota(product.shape, 0), iota(product.shape, 1)
    own_block = (row_of % chips) == (slot_of // X_ROWS)
    wanted = jnp.sum(jnp.where(own_block, product * jnp.where(row_of < chips, 256.0, 1.0), 0.0), axis=0, keepdims=True) - 1.0
    row_in_block = jnp.clip(wanted.astype(I32) - low, 0, rows - 1)
    local[...] = jnp.broadcast_to(row_in_block >> 3, local.shape)
    to_smem = pltpu.make_async_copy(local, local_smem, small_sem)
    to_smem.start()
    remainder = column((row_in_block & 7).astype(F32)).astype(I32)
    wanted_col = column(wanted)
    earlier = iota((slots, slots), 0) < iota((slots, slots), 1)
    repeated = jnp.max(jnp.where((wanted_col == wanted) & earlier, 1.0, 0.0), axis=0, keepdims=True)
    first_list = jnp.where(repeated > 0.0, -1.0, wanted)
    hot_row, hot_col = iota((X_ROWS, X_ROWS * 8), 0), iota((X_ROWS, X_ROWS * 8), 1)
    for copy in table_copies:
        copy.wait()
    to_smem.wait()
    for step in order + [0]:
        def load(s, _, base=step * X_ROWS):
            for j in range(8):
                k = s * 8 + j
                slabs[k] = table[jnp.clip(local_smem[0, base + k], 0, table.shape[0] - 1)]
            return 0
        lax.fori_loop(0, X_ROWS // 8, load, 0)
        pick = jnp.where(hot_col == hot_row * 8 + remainder[step * X_ROWS:(step + 1) * X_ROWS], 1.0, 0.0).astype(BF16)
        x_own[step] = jnp.dot(pick, slabs[...].reshape(X_ROWS * 8, hidden), preferred_element_type=F32).astype(BF16)
        if step:
            send(x_own.at[step], x_in.at[me], x_send.at[step], x_recv.at[step], device_at(step))
        else:
            send(x_own.at[0], x_in.at[me], xf_send.at[0], xf_recv.at[0], partner)
            x_in[me] = x_own[0]

    key = jnp.where(first_list >= 0.0, first_list, float(n * rows))
    key_col = column(key)
    rank = jnp.sum(jnp.where((key_col < key) | ((key_col == key) & earlier), 1.0, 0.0), axis=0, keepdims=True)
    rank_col = column(rank)
    first_col = column(first_list)
    sorted_list = jnp.sum(jnp.where(rank_col == iota((slots, slots), 1).astype(F32), first_col, 0.0), axis=0, keepdims=True)
    target_ref[...] = jnp.broadcast_to(jnp.where(sorted_list >= 0.0, sorted_list - low.astype(F32), float(n * rows)).astype(I32), target_ref.shape)
    ids = ids_ref[...]
    all_hots = one_hots(within(ids, chip * CORES * rows, (chip + 1) * CORES * rows), None, DY_ROWS)
    for i in range(n):
        code = (ids[i:i + 1] + 2).astype(F32)
        row_ids = jnp.sum(all_hots[i * DY_ROWS:(i + 1) * DY_ROWS] * code, axis=1, keepdims=True) - 2.0
        picks[i] = jnp.where(row_ids == first_list, 1.0, 0.0).astype(BF16)
        spots[i] = jnp.where(row_ids == sorted_list, 1.0, 0.0).astype(BF16)
    gain32 = wide(g_ref[...])
    x_rows = x_own[...].reshape(slots, hidden)

    def dx_of(block):
        h = jnp.dot(picks[block], x_rows, preferred_element_type=F32)
        r = rms(h)
        xh = h * r
        dy = dy_in[block].astype(F32)
        u = dy * gain32
        dx_all[block] = (r * (u - xh * jnp.mean(u * xh, axis=-1, keepdims=True))).astype(BF16)
        return jnp.sum(dy * xh, axis=0, keepdims=True)

    part = dx_of(me)
    for step in order:
        block = source(step) * CORES + core
        remote(dy_in.at[block], dy_in.at[block], dy_send.at[step], dy_recv.at[step], partner).wait_recv()
        send(dy_in.at[block], dy_in.at[block], dyf_send.at[step], dyf_recv.at[step], partner)
        part = part + dx_of(block)
    for step in [0] + order:
        block = source(step) * CORES + 1 - core
        remote(dy_in.at[block], dy_in.at[block], dyf_send.at[step], dyf_recv.at[step], partner).wait_recv()
        part = part + dx_of(block)
    dg_parts[me] = part
    length = n * DY_ROWS
    sums_ref[...] = lax.dot_general(spots[...].reshape(length, slots), dx_all[...].reshape(length, hidden), TN, preferred_element_type=F32)
    for step in range(1, n):
        send(dg_parts.at[me], dg_parts.at[me], dg_send.at[step], dg_recv.at[step], lax.rem(me + step, n))

    even, odd = ids_ref[pl.ds(chip * CORES, 1)], ids_ref[pl.ds(chip * CORES + 1, 1)]
    here_even, here_odd = even_first[0:1], odd_first[0:1]
    even_mask = jnp.concatenate([within(even, i * rows, (i + 1) * rows) for i in range(n)], axis=0) * here_even
    odd_mask = jnp.concatenate([within(odd, i * rows, (i + 1) * rows) for i in range(n)], axis=0) * here_odd
    pad = jnp.zeros((6, even.shape[1]), F32)
    product = unique_lists(even_mask, odd_mask, jnp.concatenate(halves(even) + (pad,), axis=0), jnp.concatenate(halves(odd) + (pad,), axis=0), X_ROWS)
    held = product[0:1] * 256.0 + product[1:2] - 1.0
    pick = jnp.where(column(my_ids.astype(F32)) == held, 1.0, 0.0).astype(BF16)
    most = jnp.zeros((1, 1), F32)
    for i in range(n):
        count = within(near_even, i * rows, i * rows + rows) * even_first + within(near_odd, i * rows, i * rows + rows) * odd_first
        most = jnp.maximum(most, jnp.max(jnp.sum(count, axis=1, keepdims=True) * (1.0 / X_ROWS), axis=0, keepdims=True))
    for c in range(chips):
        count = jnp.sum(within(ids, c * CORES * rows, (c + 1) * CORES * rows), axis=1, keepdims=True)
        most = jnp.maximum(most, jnp.max(count * (1.0 / DY_ROWS), axis=0, keepdims=True))
    over_ref[0, 0] = jnp.where(most > 1.0005, 1, 0)[0, 0]
    for step in order:
        block = source(step) * CORES + core
        remote(x_in.at[block], x_in.at[block], x_send.at[step], x_recv.at[step], partner).wait_recv()
        send(x_in.at[block], x_in.at[block], xf_send.at[step], xf_recv.at[step], partner)
    for step in range(1, n):
        block = dg_parts.at[lax.rem(me + n - step, n)]
        remote(block, block, dg_send.at[step], dg_recv.at[step], partner).wait_recv()
    total = dg_parts[0]
    for i in range(1, n):
        total = total + dg_parts[i]
    dg_ref[...] = total
    for step in [0] + order:
        block = source(step) * CORES + 1 - core
        remote(x_in.at[block], x_in.at[block], xf_send.at[step], xf_recv.at[step], partner).wait_recv()
    xpos_ref[...] = jnp.dot(pick, x_in[...].reshape(n * X_ROWS, hidden), preferred_element_type=F32).astype(BF16)
    for copy in sent:
        copy.wait_send()


def finish_kernel(zero_rows, target_ref, xpos_ref, sums_ref, g_ref, dg_in, y_ref, de_ref, dg_ref, zeros, targets, zero_sem, row_sem, small_sem):
    blocks = de_ref.shape[0] // zero_rows
    slots = sums_ref.shape[0]
    zeros[...] = jnp.zeros_like(zeros)

    def zero_copy(i):
        return pltpu.make_async_copy(zeros, de_ref.at[pl.ds(pl.multiple_of(i * zero_rows, 8), zero_rows)], zero_sem.at[i])

    for i in range(blocks):
        zero_copy(i).start()
    to_smem = pltpu.make_async_copy(target_ref, targets, small_sem)
    to_smem.start()
    gain = wide(g_ref[...]).astype(BF16)
    h = xpos_ref[...].astype(F32)
    y_ref[...] = (h * rms(h)).astype(BF16) * gain
    for i in range(dg_ref.shape[0]):
        dg_ref[i:i + 1] = dg_in[:, i * 128:(i + 1) * 128]
    to_smem.wait()

    def row_copy(k):
        return pltpu.make_async_copy(sums_ref.at[pl.ds(k, 1)], de_ref.at[pl.ds(targets[0, k], 1)], row_sem)

    def block(i, k):
        zero_copy(i).wait()

        def put(k):
            row_copy(k).start()
            return k + 1
        return lax.while_loop(lambda k: (k < slots) & (targets[0, jnp.minimum(k, slots - 1)] < (i + 1) * zero_rows), put, k)

    count = lax.fori_loop(0, blocks, block, 0)

    def done(k, _):
        row_copy(k).wait()
        return 0

    lax.fori_loop(0, count, done, 0)


def vmem():
    return pl.BlockSpec(memory_space=pltpu.VMEM)


def smem():
    return pl.BlockSpec(memory_space=pltpu.SMEM)


def anywhere():
    return pl.BlockSpec(memory_space=pl.ANY)


def dma(*shape):
    return pltpu.SemaphoreType.DMA(shape)


def pair_exchange_kernel(n, x_out, dy_out, x_in, dy_in, dg_ref, dg_parts, x_send, x_recv, dy_send, dy_recv, dg_send, dg_recv):
    me = lax.axis_index('tp')
    dp = lax.axis_index('dp')
    barrier = pltpu.get_barrier_semaphore()
    for step in range(1, n):
        pl.semaphore_signal(barrier, inc=1, device_id=(dp, lax.rem(me + step, n)), device_id_type=MESH)
    pl.semaphore_wait(barrier, n - 1)

    def copies(src, dst, send_sem, recv_sem, step):
        peer = lax.rem(me + step, n)
        return pltpu.make_async_remote_copy(
            src_ref=src.at[peer], dst_ref=dst.at[me], send_sem=send_sem.at[step], recv_sem=recv_sem.at[step],
            device_id=(dp, peer), device_id_type=MESH)

    def arrival(dst, send_sem, recv_sem, step):
        source = lax.rem(me + n - step, n)
        return pltpu.make_async_remote_copy(
            src_ref=dst.at[source], dst_ref=dst.at[source], send_sem=send_sem.at[step], recv_sem=recv_sem.at[step],
            device_id=(dp, source), device_id_type=MESH)

    x_copies = [copies(x_out, x_in, x_send, x_recv, step) for step in range(1, n)]
    for copy in x_copies:
        copy.start()
    dy_copies = [copies(dy_out, dy_in, dy_send, dy_recv, step) for step in range(1, n)]
    for copy in dy_copies:
        copy.start()
    x_in[me] = x_out[me]
    dy_in[me] = dy_out[me]

    def dg_of(block):
        h = x_in[block].astype(F32)
        return jnp.sum(dy_out[block].astype(F32) * (h * rms(h)), axis=0, keepdims=True)

    for step in range(1, n):
        arrival(x_in, x_send, x_recv, step).wait_recv()
    dg_parts[me] = lax.fori_loop(1, n, lambda i, total: total + dg_of(i), dg_of(0))

    def dg_copy(step):
        return pltpu.make_async_remote_copy(
            src_ref=dg_parts.at[me], dst_ref=dg_parts.at[me], send_sem=dg_send.at[step], recv_sem=dg_recv.at[step],
            device_id=(dp, lax.rem(me + step, n)), device_id_type=MESH)

    dg_copies = [dg_copy(step) for step in range(1, n)]
    for copy in dg_copies:
        copy.start()
    for step in range(1, n):
        arrival(dy_in, dy_send, dy_recv, step).wait_recv()
    for step in range(1, n):
        arrival(dg_parts, dg_send, dg_recv, step).wait_recv()
    for i in range(n):
        dg_ref[i:i + 1] = dg_parts[i]
    for copy in x_copies + dy_copies + dg_copies:
        copy.wait_send()


def any_path(n, ids, table_block, norm_gain, grad_block):
    rows, hidden = table_block.shape
    positions = ids.shape[1]
    cap = positions
    me = lax.axis_index('tp')
    before = (iota((positions, positions), 0) < iota((positions, positions), 1)).astype(I32)

    def slots_of(mask):
        return jnp.sum(mask.astype(I32)[:, :, None] * before[None], axis=1)

    local = ids - me * rows
    mine = (local >= 0) & (local < rows)
    slot = slots_of(mine)
    hit = mine[:, None, :] & (slot[:, None, :] == jnp.arange(cap)[None, :, None])
    wanted = jnp.sum(jnp.where(hit, local[:, None, :] + 1, 0), axis=-1).reshape(n * cap) - 1
    x_own = jnp.take(table_block, jnp.maximum(wanted, 0), axis=0)
    my_ids = lax.dynamic_index_in_dim(ids, me, 0, keepdims=True)
    starts = jnp.arange(n, dtype=I32)[:, None] * rows
    theirs = (my_ids >= starts) & (my_ids < starts + rows)
    their_slot = slots_of(theirs)
    hot = theirs[:, None, :] & (their_slot[:, None, :] == jnp.arange(cap)[None, :, None])
    dy_out = jnp.dot(hot.reshape(n * cap, positions).astype(BF16), grad_block.reshape(positions, hidden))
    slot_of = jnp.sum(jnp.where(theirs, jnp.arange(n)[:, None] * cap + their_slot, 0), axis=0)
    x_in, dy_in, dg = pl.pallas_call(
        functools.partial(pair_exchange_kernel, n),
        out_shape=(jax.ShapeDtypeStruct((n, cap, hidden), BF16), jax.ShapeDtypeStruct((n, cap, hidden), BF16), jax.ShapeDtypeStruct((n, hidden), F32)),
        in_specs=[vmem(), vmem()],
        out_specs=(vmem(), vmem(), vmem()),
        scratch_shapes=[pltpu.VMEM((n, 1, hidden), F32)] + [dma(n)] * 6,
        compiler_params=pltpu.CompilerParams(collective_id=1, has_side_effects=True, vmem_limit_bytes=LIMIT),
        name='exchange_pairs',
    )(x_own.reshape(n, cap, hidden), dy_out.reshape(n, cap, hidden))
    h = jnp.take(x_in.reshape(n * cap, hidden), slot_of, axis=0).astype(F32)
    y = (h * rms(h)).astype(BF16) * norm_gain
    h = x_own.astype(F32)
    r = rms(h)
    xh = h * r
    u = dy_in.reshape(n * cap, hidden).astype(F32) * norm_gain.astype(F32)
    dx = (r * (u - xh * jnp.mean(u * xh, axis=-1, keepdims=True))).astype(BF16)
    grad_table = jax.ops.segment_sum(dx.astype(F32), jnp.where(wanted >= 0, wanted, rows), num_segments=rows)
    return y.reshape(grad_block.shape), grad_table, jnp.sum(dg, axis=0)


def call(kernel, name, out_shape, in_specs, out_specs, scratch_shapes, flops, limit, aliases=None, **params):
    return pl.pallas_call(
        kernel, out_shape=out_shape, in_specs=in_specs, out_specs=out_specs, scratch_shapes=scratch_shapes, name=name,
        input_output_aliases=aliases or {}, cost_estimate=pl.CostEstimate(flops=flops, bytes_accessed=2**24, transcendentals=0),
        compiler_params=pltpu.CompilerParams(vmem_limit_bytes=limit * 2**20, **params))


def device_step(n, token_ids, table_block, norm_gain, grad_block):
    positions = grad_block.shape[0] * grad_block.shape[1]
    rows, hidden = table_block.shape
    ids = token_ids.reshape(n, positions)
    chips = n // CORES
    slots = chips * X_ROWS
    zero_rows = divisor(rows, ZERO_ROWS)
    shape = jax.ShapeDtypeStruct
    gain = norm_gain.reshape(hidden // 128, 128)
    slabs = rows // 8
    xpos, sums, dg, target, over = call(
        functools.partial(exchange_kernel, n, rows), 'exchange',
        (shape((positions, hidden), BF16), shape((slots, hidden), F32), shape((1, hidden), F32), shape((8, slots), I32), shape((1, 1), I32)),
        [vmem(), anywhere(), vmem(), vmem()], (vmem(),) * 4 + (smem(),),
        [pltpu.VMEM((slabs, 8, hidden), BF16), pltpu.VMEM((X_ROWS, 8, hidden), BF16), pltpu.VMEM((8, slots), I32), pltpu.SMEM((8, slots), I32),
         pltpu.VMEM((chips, X_ROWS, hidden), BF16), pltpu.VMEM((n, X_ROWS, hidden), BF16), pltpu.VMEM((chips, DY_ROWS, hidden), BF16),
         pltpu.VMEM((n, DY_ROWS, hidden), BF16), pltpu.VMEM((n, DY_ROWS, slots), BF16), pltpu.VMEM((n, DY_ROWS, slots), BF16),
         pltpu.VMEM((n, DY_ROWS, hidden), BF16), pltpu.VMEM((n, 1, hidden), F32), dma(max(d for d in range(1, 11) if slabs % d == 0)), pltpu.SemaphoreType.DMA]
        + [dma(chips)] * 8 + [dma(n)] * 2, 10**9, 48, collective_id=0, has_side_effects=True)(
            ids, table_block.reshape(slabs, 8, hidden), grad_block.reshape(positions, hidden), gain)
    y, grad_table, dg = call(
        functools.partial(finish_kernel, zero_rows), 'finish',
        (shape((positions, hidden), BF16), shape((rows, hidden), F32), shape((hidden // 128, 128), F32)),
        [anywhere()] + [vmem()] * 4, (vmem(), anywhere(), vmem()),
        [pltpu.VMEM((zero_rows, hidden), F32), pltpu.SMEM((8, slots), I32), dma(rows // zero_rows), pltpu.SemaphoreType.DMA, pltpu.SemaphoreType.DMA],
        10**9, 36)(target, xpos, sums, gain, dg)
    result = y.reshape(grad_block.shape), grad_table, dg.reshape(hidden)

    def general(carry):
        return (jnp.zeros((), I32),) + any_path(n, ids, table_block, norm_gain, grad_block)

    return lax.while_loop(lambda carry: carry[0] > 0, general, (over[0, 0],) + result)[1:]


def solution(mesh):
    return jax.shard_map(functools.partial(device_step, mesh.shape['tp']), mesh=mesh, in_specs=(P('dp', None), P('tp', None), P(None), P('dp', 'tp', None)), out_specs=(P('dp', 'tp', None), P(('dp', 'tp'), None), P('dp')), check_vma=False)
```

time: 133 us -> 42.2 us (0.32)
  waiting for transfers between devices: 44.5 us -> 0 us
  Pallas kernels: 0 us -> 40.3 us
  other arithmetic: 39.9 us -> 0 us
  blocking collectives: 17.1 us -> 0 us
  local copies, waits for them, and re-layouts: 17.1 us -> 0.01 us
  between operations: 14.1 us -> 0.87 us
    pallas_call x0 -> x2, Pallas kernels: none -> 40.3 us  [the longest x1 27.9 us: device_step(): call(functools.partial(exchange_kernel, n, rows), 'exchange', (shape((pos...]
    reduce_scatter x1 -> x0, waiting for transfers between devices: 33.4 us -> none  [device_step(): lax.psum_scatter(partial_rows, 'tp', scatter_dimension=1, tiled=True)]
    scatter-add x1 -> x0, other arithmetic: 28.1 us -> none  [device_step(): jax.ops.segment_sum(grad_all.astype(jnp.float32).reshape(-1, hidden_size)...]
    psum x1 -> x0, blocking collectives: 17.1 us -> none  [device_step(): grad_gain = lax.psum(gain_part, 'tp')]
    gather x1 -> x0, local copies, waits for them, and re-layouts: 16.6 us -> none  [device_step(): looked_up = jnp.take(table_block, jnp.where(owned, local_ids, 0), axis=0)]
    all_gather x1 -> x0, waiting for transfers between devices: 11 us -> none  [device_step(): grad_all = lax.all_gather(grad_in, 'tp', axis=1, tiled=True)]
    select_n x2 -> x0, other arithmetic: 4.11 us -> none  [the longest x1 4.1 us: device_step(): jnp.where(owned[:, :, None], looked_up, jnp.zeros((), jnp.bfloat16))]
    reduce_sum x2 -> x0, other arithmetic: 2.7 us -> none  [the longest x1 1.47 us: norm_pass(): gain_part = jnp.sum(grad_f32 * x_hat, axis=(0, 1))]
  transfers between devices with their start and end apart: 2 -> 0, of which waited for: 2 -> 0; matrix products, arithmetic and copies ran while one was open for 2% -> 0% of each run, Pallas kernels for 0% -> 0%
where the time goes in v3:
time: 42.2 us; the launch traced here: 42 us
  Pallas kernels  40.3 us (95%)
  between operations  0.87 us (2%)
  loops' own time  0.85 us (2%)
    pallas_call x1, Pallas kernels, device_step(): call(functools.partial(exchange_kernel, n, rows), 'exchange', (shape((pos...  27.9 us
    pallas_call x1, Pallas kernels, device_step(): call(functools.partial(finish_kernel, zero_rows), 'finish', (shape((posit...  12.4 us
    another operation x1, loops' own time, device_step(): lax.while_loop(lambda carry: carry[0] > 0, general, (over[0, 0],) + result)  0.85 us

profile of v3, /device:TPU:113, one launch (start us, length us, event | category | flops | bytes accessed | tf_op | source)
XLA Modules:
  0.0 42.0 jit_solution(4724414528572973231)
XLA Ops:
  0.6 0.0 copy-start.4
  0.6 0.0 copy-start.2
  0.7 0.0 copy-start.5
  0.7 27.9 %exchange.1 = (bf16[128,2048]{1,0:T(8,128)(2,1)S(1)}, f32[160,2048]{1,0:T(8,128)S(1)}, f32[1,2048]{1,0:T(1,128)S(1)}, s32[8,160]{1,0:T(8,128)S(1)}, s32[1,1]{1,0:T(1,128)}) custom-call(s32[8,128]{1,0:T(8,128)} %bitcast.46, bf16[500,8,2048]{2,1,0:T(8,128)(2,1)} %bitcast.41, bf16[128,2048]{1,0:T(8,128)(2,1)} %bitcast.43, bf16[16,128]{1,0:T(8,128)(2,1)} %bitcast.44), custom_call_target="tpu_custom_call" | custom-call | flops 1000000000 | bytes 16777216 | tf_op jit(solution)/shard_map/exchange/pallas_call | solution.py:420
  28.5 0.0 copy-done.4
  28.5 12.4 %finish.1 = (bf16[128,2048]{1,0:T(8,128)(2,1)}, f32[4000,2048]{1,0:T(8,128)}, f32[16,128]{1,0:T(8,128)}) custom-call(s32[8,160]{1,0:T(8,128)S(1)} %get-tuple-element.55.target_ref, bf16[128,2048]{1,0:T(8,128)(2,1)S(1)} %get-tuple-element.56.xpos_ref, f32[160,2048]{1,0:T(8,128)S(1)} %get-tuple-element.57.sums_ref, bf16[16,128]{1,0:T(8,128)(2,1)S(1)} %bitcast.45, ...), custom_call_target="tpu_custom_call" | custom-call | flops 1000000000 | bytes 16777216 | tf_op jit(solution)/shard_map/finish/pallas_call | solution.py:430
  41.0 0.0 copy-done.2
  41.0 0.0 copy-done.5
  41.0 0.8 %while.13 = (s32[]{:T(128)}, bf16[1,128,2048]{2,1,0:T(8,128)(2,1)}, f32[4000,2048]{1,0:T(8,128)}, f32[2048]{0:T(1024)}, s32[8,128]{1,0:T(8,128)S(1)}, /*index=5*...) while((s32[]{:T(128)}, bf16[1,128,2048]{2,1,0:T(8,128)(2,1)}, ...), condition=%region_10.11_spmd, body=%region_0.10_spmd | while | flops 588850304 | bytes 120461624 | solution.py:441
Async XLA Ops:
  0.6 27.9 %copy-start.4 = (bf16[2048]{0:T(1024)(128)(2,1)S(1)}, bf16[2048]{0:T(1024)(128)(2,1)}, u32[]{:S(2)}) copy-start(bf16[2048]{0:T(1024)(128)(2,1)} %param.8) | copy-start | bytes 12292
  0.6 40.3 %copy-start.2 = (bf16[1,128,2048]{2,1,0:T(8,128)(2,1)S(1)}, bf16[1,128,2048]{2,1,0:T(8,128)(2,1)}, u32[]{:S(2)}) copy-start(bf16[1,128,2048]{2,1,0:T(8,128)(2,1)} %param.9) | copy-start | bytes 1572868
  0.7 40.3 %copy-start.5 = (s32[1,1024]{1,0:T(1,128)S(1)}, s32[1,1024]{1,0:T(1,128)}, u32[]{:S(2)}) copy-start(s32[1,1024]{1,0:T(1,128)} %param.6) | copy-start | bytes 12292

commit v4 on v3

--- a/solution.py
+++ b/solution.py
@@ -11,7 +11,7 @@
 CORES = 2
 X_ROWS = 40
 DY_ROWS = 56
-ZERO_ROWS = 80
+ZERO_ROWS = 160
 MESH = pl.DeviceIdType.MESH
 F32 = jnp.float32
 BF16 = jnp.bfloat16
@@ -79,9 +79,9 @@
     return jnp.where((ids >= low) & (ids < high), 1.0, 0.0)
 
 
-def exchange_kernel(n, rows, ids_ref, table_hbm, dy_own, g_ref, xpos_ref, sums_ref, dg_ref, target_ref, over_ref,
-                    table, slabs, local, local_smem, x_own, x_in, dy_out, dy_in, picks, spots, dx_all, dg_parts,
-                    table_sem, small_sem, x_send, x_recv, xf_send, xf_recv, dy_send, dy_recv, dyf_send, dyf_recv, dg_send, dg_recv):
+def exchange_kernel(n, rows, ids_hbm, table_hbm, dy_hbm, g_hbm, xpos_ref, sums_ref, dg_ref, target_ref, over_ref,
+                    ids_ref, g_ref, dy_own, table, slabs, local, local_smem, x_own, x_in, dy_out, dy_in, picks, spots, dx_all, dg_parts,
+                    table_sem, small_sem, own_sem, x_send, x_recv, xf_send, xf_recv, dy_send, dy_recv, dyf_send, dyf_recv, dg_send, dg_recv):
     chips = n // CORES
     me = lax.axis_index('tp')
     dp = lax.axis_index('dp')
@@ -92,12 +92,14 @@
     barrier = pltpu.get_barrier_semaphore()
     for step in range(1, n):
         pl.semaphore_signal(barrier, inc=1, device_id=(dp, lax.rem(me + step, n)), device_id_type=MESH)
+    load_ids = pltpu.make_async_copy(ids_hbm, ids_ref, own_sem.at[0])
+    load_dy = pltpu.make_async_copy(dy_hbm, dy_own, own_sem.at[1])
+    load_gain = pltpu.make_async_copy(g_hbm, g_ref, own_sem.at[2])
+    for copy in (load_ids, load_dy, load_gain):
+        copy.start()
     pieces = table_sem.shape[0]
     piece = table_hbm.shape[0] // pieces
     table_copies = [pltpu.make_async_copy(table_hbm.at[pl.ds(i * piece, piece)], table.at[pl.ds(i * piece, piece)], table_sem.at[i]) for i in range(pieces)]
-    for copy in table_copies:
-        copy.start()
-
     def remote(src, dst, send_sem, recv_sem, device):
         return pltpu.make_async_remote_copy(src_ref=src, dst_ref=dst, send_sem=send_sem, recv_sem=recv_sem, device_id=(dp, device), device_id_type=MESH)
 
@@ -114,15 +116,21 @@
     def device_at(step):
         return lax.rem(chip + step, chips) * CORES + core
 
-    order = [1, chips - 1] + list(range(2, chips - 1))
+    order = list(range(2, chips - 1)) + [1, chips - 1]
     low = me * rows
 
+    load_ids.wait()
     my_ids = ids_ref[pl.ds(me, 1)]
     near = [lax.rem(chip + step, chips) for step in range(chips)]
     masks = jnp.concatenate([within(my_ids, c * CORES * rows, (c + 1) * CORES * rows) for c in near], axis=0)
     hots = one_hots(masks, None, DY_ROWS).astype(BF16)
+    load_dy.wait()
+    load_gain.wait()
+    for copy in table_copies:
+        copy.start()
+    lists = jnp.dot(hots, dy_own[...], preferred_element_type=F32).astype(BF16)
     for step in range(chips):
-        dy_out[step] = jnp.dot(hots[step * DY_ROWS:(step + 1) * DY_ROWS], dy_own[...], preferred_element_type=F32).astype(BF16)
+        dy_out[step] = lists[step * DY_ROWS:(step + 1) * DY_ROWS]
     pl.semaphore_wait(barrier, n - 1)
     for step in order:
         send(dy_out.at[step], dy_in.at[me], dy_send.at[step], dy_recv.at[step], device_at(step))
@@ -247,7 +255,7 @@
         copy.wait_send()
 
 
-def finish_kernel(zero_rows, target_ref, xpos_ref, sums_ref, g_ref, dg_in, y_ref, de_ref, dg_ref, zeros, targets, zero_sem, row_sem, small_sem):
+def finish_kernel(zero_rows, target_ref, xpos_ref, sums_ref, g_ref, dg_in, y_hbm, de_ref, dg_hbm, zeros, targets, y_ref, dg_ref, zero_sem, row_sem, small_sem, out_sem):
     blocks = de_ref.shape[0] // zero_rows
     slots = sums_ref.shape[0]
     zeros[...] = jnp.zeros_like(zeros)
@@ -264,6 +272,9 @@
     y_ref[...] = (h * rms(h)).astype(BF16) * gain
     for i in range(dg_ref.shape[0]):
         dg_ref[i:i + 1] = dg_in[:, i * 128:(i + 1) * 128]
+    outs = [pltpu.make_async_copy(y_ref, y_hbm, out_sem.at[0]), pltpu.make_async_copy(dg_ref, dg_hbm, out_sem.at[1])]
+    for copy in outs:
+        copy.start()
     to_smem.wait()
 
     def row_copy(k):
@@ -284,6 +295,8 @@
         return 0
 
     lax.fori_loop(0, count, done, 0)
+    for copy in outs:
+        copy.wait()
 
 
 def vmem():
@@ -420,18 +433,19 @@
     xpos, sums, dg, target, over = call(
         functools.partial(exchange_kernel, n, rows), 'exchange',
         (shape((positions, hidden), BF16), shape((slots, hidden), F32), shape((1, hidden), F32), shape((8, slots), I32), shape((1, 1), I32)),
-        [vmem(), anywhere(), vmem(), vmem()], (vmem(),) * 4 + (smem(),),
-        [pltpu.VMEM((slabs, 8, hidden), BF16), pltpu.VMEM((X_ROWS, 8, hidden), BF16), pltpu.VMEM((8, slots), I32), pltpu.SMEM((8, slots), I32),
+        [anywhere()] * 4, (vmem(),) * 4 + (smem(),),
+        [pltpu.VMEM((n, positions), I32), pltpu.VMEM((hidden // 128, 128), BF16), pltpu.VMEM((positions, hidden), BF16), pltpu.VMEM((slabs, 8, hidden), BF16), pltpu.VMEM((X_ROWS, 8, hidden), BF16), pltpu.VMEM((8, slots), I32), pltpu.SMEM((8, slots), I32),
          pltpu.VMEM((chips, X_ROWS, hidden), BF16), pltpu.VMEM((n, X_ROWS, hidden), BF16), pltpu.VMEM((chips, DY_ROWS, hidden), BF16),
          pltpu.VMEM((n, DY_ROWS, hidden), BF16), pltpu.VMEM((n, DY_ROWS, slots), BF16), pltpu.VMEM((n, DY_ROWS, slots), BF16),
-         pltpu.VMEM((n, DY_ROWS, hidden), BF16), pltpu.VMEM((n, 1, hidden), F32), dma(max(d for d in range(1, 11) if slabs % d == 0)), pltpu.SemaphoreType.DMA]
+         pltpu.VMEM((n, DY_ROWS, hidden), BF16), pltpu.VMEM((n, 1, hidden), F32), dma(max(d for d in range(1, 11) if slabs % d == 0)), pltpu.SemaphoreType.DMA, dma(3)]
         + [dma(chips)] * 8 + [dma(n)] * 2, 10**9, 48, collective_id=0, has_side_effects=True)(
             ids, table_block.reshape(slabs, 8, hidden), grad_block.reshape(positions, hidden), gain)
     y, grad_table, dg = call(
         functools.partial(finish_kernel, zero_rows), 'finish',
         (shape((positions, hidden), BF16), shape((rows, hidden), F32), shape((hidden // 128, 128), F32)),
-        [anywhere()] + [vmem()] * 4, (vmem(), anywhere(), vmem()),
-        [pltpu.VMEM((zero_rows, hidden), F32), pltpu.SMEM((8, slots), I32), dma(rows // zero_rows), pltpu.SemaphoreType.DMA, pltpu.SemaphoreType.DMA],
+        [anywhere()] + [vmem()] * 4, (anywhere(),) * 3,
+        [pltpu.VMEM((zero_rows, hidden), F32), pltpu.SMEM((8, slots), I32), pltpu.VMEM((positions, hidden), BF16), pltpu.VMEM((hidden // 128, 128), F32),
+         dma(rows // zero_rows), pltpu.SemaphoreType.DMA, pltpu.SemaphoreType.DMA, dma(2)],
         10**9, 36)(target, xpos, sums, gain, dg)
     result = y.reshape(grad_block.shape), grad_table, dg.reshape(hidden)
 

time: 42.2 us -> 40.2 us (0.953)
  Pallas kernels: 40.3 us -> 38.4 us
    pallas_call x1, Pallas kernels: 27.9 us -> 26.7 us  [device_step(): call(functools.partial(exchange_kernel, n, rows), 'exchange', (shape((pos...]
    pallas_call x1, Pallas kernels: 12.4 us -> 11.7 us  [device_step(): call(functools.partial(finish_kernel, zero_rows), 'finish', (shape((posit...]
where the time goes in v4:
time: 40.2 us; the launch traced here: 40.1 us
  Pallas kernels  38.4 us (96%)
  between operations  0.87 us (2%)
  loops' own time  0.85 us (2%)
    pallas_call x1, Pallas kernels, device_step(): call(functools.partial(exchange_kernel, n, rows), 'exchange', (shape((pos...  26.7 us
    pallas_call x1, Pallas kernels, device_step(): call(functools.partial(finish_kernel, zero_rows), 'finish', (shape((posit...  11.7 us
    another operation x1, loops' own time, device_step(): lax.while_loop(lambda carry: carry[0] > 0, general, (over[0, 0],) + result)  0.85 us

profile of v4, /device:TPU:113, one launch (start us, length us, event | category | flops | bytes accessed | tf_op | source)
XLA Modules:
  0.0 40.1 jit_solution(2476262828354801732)
XLA Ops:
  0.6 0.0 copy-start.4
  0.6 0.0 copy-start.2
  0.7 0.0 copy-start.5
  0.7 26.7 %exchange.1 = (bf16[128,2048]{1,0:T(8,128)(2,1)S(1)}, f32[160,2048]{1,0:T(8,128)S(1)}, f32[1,2048]{1,0:T(1,128)S(1)}, s32[8,160]{1,0:T(8,128)S(1)}, s32[1,1]{1,0:T(1,128)}) custom-call(s32[8,128]{1,0:T(8,128)} %bitcast.46, bf16[500,8,2048]{2,1,0:T(8,128)(2,1)} %bitcast.41, bf16[128,2048]{1,0:T(8,128)(2,1)} %bitcast.43, bf16[16,128]{1,0:T(8,128)(2,1)} %bitcast.44), custom_call_target="tpu_custom_call" | custom-call | flops 1000000000 | bytes 16777216 | tf_op jit(solution)/shard_map/exchange/pallas_call | solution.py:433
  27.3 0.0 copy-done.4
  27.3 11.7 %finish.1 = (bf16[128,2048]{1,0:T(8,128)(2,1)}, f32[4000,2048]{1,0:T(8,128)}, f32[16,128]{1,0:T(8,128)}) custom-call(s32[8,160]{1,0:T(8,128)S(1)} %get-tuple-element.55.target_ref, bf16[128,2048]{1,0:T(8,128)(2,1)S(1)} %get-tuple-element.56.xpos_ref, f32[160,2048]{1,0:T(8,128)S(1)} %get-tuple-element.57.sums_ref, bf16[16,128]{1,0:T(8,128)(2,1)S(1)} %bitcast.45, ...), custom_call_target="tpu_custom_call" | custom-call | flops 1000000000 | bytes 16777216 | tf_op jit(solution)/shard_map/finish/pallas_call | solution.py:443
  39.1 0.0 copy-done.2
  39.1 0.0 copy-done.5
  39.1 0.8 %while.13 = (s32[]{:T(128)}, bf16[1,128,2048]{2,1,0:T(8,128)(2,1)}, f32[4000,2048]{1,0:T(8,128)}, f32[2048]{0:T(1024)}, s32[8,128]{1,0:T(8,128)S(1)}, /*index=5*...) while((s32[]{:T(128)}, bf16[1,128,2048]{2,1,0:T(8,128)(2,1)}, ...), condition=%region_10.11_spmd, body=%region_0.10_spmd | while | flops 588850304 | bytes 120461624 | solution.py:455
Async XLA Ops:
  0.6 26.7 %copy-start.4 = (bf16[2048]{0:T(1024)(128)(2,1)S(1)}, bf16[2048]{0:T(1024)(128)(2,1)}, u32[]{:S(2)}) copy-start(bf16[2048]{0:T(1024)(128)(2,1)} %param.8) | copy-start | bytes 12292
  0.6 38.4 %copy-start.2 = (bf16[1,128,2048]{2,1,0:T(8,128)(2,1)S(1)}, bf16[1,128,2048]{2,1,0:T(8,128)(2,1)}, u32[]{:S(2)}) copy-start(bf16[1,128,2048]{2,1,0:T(8,128)(2,1)} %param.9) | copy-start | bytes 1572868
  0.7 38.4 %copy-start.5 = (s32[1,1024]{1,0:T(1,128)S(1)}, s32[1,1024]{1,0:T(1,128)}, u32[]{:S(2)}) copy-start(s32[1,1024]{1,0:T(1,128)} %param.6) | copy-start | bytes 12292

commit v5 on v4

--- a/solution.py
+++ b/solution.py
@@ -79,8 +79,8 @@
     return jnp.where((ids >= low) & (ids < high), 1.0, 0.0)
 
 
-def exchange_kernel(n, rows, ids_hbm, table_hbm, dy_hbm, g_hbm, xpos_ref, sums_ref, dg_ref, target_ref, over_ref,
-                    ids_ref, g_ref, dy_own, table, slabs, local, local_smem, x_own, x_in, dy_out, dy_in, picks, spots, dx_all, dg_parts,
+def exchange_kernel(n, rows, ids_hbm, table_hbm, dy_hbm, g_hbm, xpos_ref, sums_ref, dg_ref, target_ref, over_hbm,
+                    over_ref, ids_ref, g_ref, dy_own, table, slabs, local, local_smem, x_own, x_in, dy_out, dy_in, picks, spots, dx_all, dg_parts,
                     table_sem, small_sem, own_sem, x_send, x_recv, xf_send, xf_recv, dy_send, dy_recv, dyf_send, dyf_recv, dg_send, dg_recv):
     chips = n // CORES
     me = lax.axis_index('tp')
@@ -236,6 +236,8 @@
         count = jnp.sum(within(ids, c * CORES * rows, (c + 1) * CORES * rows), axis=1, keepdims=True)
         most = jnp.maximum(most, jnp.max(count * (1.0 / DY_ROWS), axis=0, keepdims=True))
     over_ref[0, 0] = jnp.where(most > 1.0005, 1, 0)[0, 0]
+    put_over = pltpu.make_async_copy(over_ref, over_hbm, own_sem.at[0])
+    put_over.start()
     for step in order:
         block = source(step) * CORES + core
         remote(x_in.at[block], x_in.at[block], x_send.at[step], x_recv.at[step], partner).wait_recv()
@@ -253,6 +255,7 @@
     xpos_ref[...] = jnp.dot(pick, x_in[...].reshape(n * X_ROWS, hidden), preferred_element_type=F32).astype(BF16)
     for copy in sent:
         copy.wait_send()
+    put_over.wait()
 
 
 def finish_kernel(zero_rows, target_ref, xpos_ref, sums_ref, g_ref, dg_in, y_hbm, de_ref, dg_hbm, zeros, targets, y_ref, dg_ref, zero_sem, row_sem, small_sem, out_sem):
@@ -433,8 +436,8 @@
     xpos, sums, dg, target, over = call(
         functools.partial(exchange_kernel, n, rows), 'exchange',
         (shape((positions, hidden), BF16), shape((slots, hidden), F32), shape((1, hidden), F32), shape((8, slots), I32), shape((1, 1), I32)),
-        [anywhere()] * 4, (vmem(),) * 4 + (smem(),),
-        [pltpu.VMEM((n, positions), I32), pltpu.VMEM((hidden // 128, 128), BF16), pltpu.VMEM((positions, hidden), BF16), pltpu.VMEM((slabs, 8, hidden), BF16), pltpu.VMEM((X_ROWS, 8, hidden), BF16), pltpu.VMEM((8, slots), I32), pltpu.SMEM((8, slots), I32),
+        [anywhere()] * 4, (vmem(),) * 4 + (anywhere(),),
+        [pltpu.SMEM((1, 1), I32), pltpu.VMEM((n, positions), I32), pltpu.VMEM((hidden // 128, 128), BF16), pltpu.VMEM((positions, hidden), BF16), pltpu.VMEM((slabs, 8, hidden), BF16), pltpu.VMEM((X_ROWS, 8, hidden), BF16), pltpu.VMEM((8, slots), I32), pltpu.SMEM((8, slots), I32),
          pltpu.VMEM((chips, X_ROWS, hidden), BF16), pltpu.VMEM((n, X_ROWS, hidden), BF16), pltpu.VMEM((chips, DY_ROWS, hidden), BF16),
          pltpu.VMEM((n, DY_ROWS, hidden), BF16), pltpu.VMEM((n, DY_ROWS, slots), BF16), pltpu.VMEM((n, DY_ROWS, slots), BF16),
          pltpu.VMEM((n, DY_ROWS, hidden), BF16), pltpu.VMEM((n, 1, hidden), F32), dma(max(d for d in range(1, 11) if slabs % d == 0)), pltpu.SemaphoreType.DMA, dma(3)]

time: 40.2 us -> 39.7 us (0.988)
  Pallas kernels: 38.4 us -> 37.9 us
    pallas_call x1, Pallas kernels: 26.7 us -> 26.1 us  [device_step(): call(functools.partial(exchange_kernel, n, rows), 'exchange', (shape((pos...]
where the time goes in v5:
time: 39.7 us; the launch traced here: 39.6 us
  Pallas kernels  37.9 us (95%)
  between operations  0.87 us (2%)
  loops' own time  0.85 us (2%)
    pallas_call x1, Pallas kernels, device_step(): call(functools.partial(exchange_kernel, n, rows), 'exchange', (shape((pos...  26.1 us
    pallas_call x1, Pallas kernels, device_step(): call(functools.partial(finish_kernel, zero_rows), 'finish', (shape((posit...  11.7 us
    another operation x1, loops' own time, device_step(): lax.while_loop(lambda carry: carry[0] > 0, general, (over[0, 0],) + result)  0.85 us

profile of v5, /device:TPU:113, one launch (start us, length us, event | category | flops | bytes accessed | tf_op | source)
XLA Modules:
  0.0 39.6 jit_solution(6008917547215592184)
XLA Ops:
  0.6 0.0 copy-start.4
  0.6 0.0 copy-start.2
  0.7 0.0 copy-start.5
  0.7 26.1 %exchange.1 = (bf16[128,2048]{1,0:T(8,128)(2,1)S(1)}, f32[160,2048]{1,0:T(8,128)S(1)}, f32[1,2048]{1,0:T(1,128)S(1)}, s32[8,160]{1,0:T(8,128)S(1)}, s32[1,1]{1,0:T(1,128)}) custom-call(s32[8,128]{1,0:T(8,128)} %bitcast.46, bf16[500,8,2048]{2,1,0:T(8,128)(2,1)} %bitcast.41, bf16[128,2048]{1,0:T(8,128)(2,1)} %bitcast.43, bf16[16,128]{1,0:T(8,128)(2,1)} %bitcast.44), custom_call_target="tpu_custom_call" | custom-call | flops 1000000000 | bytes 16777216 | tf_op jit(solution)/shard_map/exchange/pallas_call | solution.py:436
  26.8 0.0 copy-done.4
  26.8 11.7 %finish.1 = (bf16[128,2048]{1,0:T(8,128)(2,1)}, f32[4000,2048]{1,0:T(8,128)}, f32[16,128]{1,0:T(8,128)}) custom-call(s32[8,160]{1,0:T(8,128)S(1)} %get-tuple-element.55.target_ref, bf16[128,2048]{1,0:T(8,128)(2,1)S(1)} %get-tuple-element.56.xpos_ref, f32[160,2048]{1,0:T(8,128)S(1)} %get-tuple-element.57.sums_ref, bf16[16,128]{1,0:T(8,128)(2,1)S(1)} %bitcast.45, ...), custom_call_target="tpu_custom_call" | custom-call | flops 1000000000 | bytes 16777216 | tf_op jit(solution)/shard_map/finish/pallas_call | solution.py:446
  38.6 0.0 copy-done.2
  38.6 0.0 copy-done.5
  38.6 0.8 %while.13 = (s32[]{:T(128)}, bf16[1,128,2048]{2,1,0:T(8,128)(2,1)}, f32[4000,2048]{1,0:T(8,128)}, f32[2048]{0:T(1024)}, s32[8,128]{1,0:T(8,128)S(1)}, /*index=5*...) while((s32[]{:T(128)}, bf16[1,128,2048]{2,1,0:T(8,128)(2,1)}, ...), condition=%region_10.11_spmd, body=%region_0.10_spmd | while | flops 588850304 | bytes 120461624 | solution.py:458
Async XLA Ops:
  0.6 26.2 %copy-start.4 = (bf16[2048]{0:T(1024)(128)(2,1)S(1)}, bf16[2048]{0:T(1024)(128)(2,1)}, u32[]{:S(2)}) copy-start(bf16[2048]{0:T(1024)(128)(2,1)} %param.8) | copy-start | bytes 12292
  0.6 37.9 %copy-start.2 = (bf16[1,128,2048]{2,1,0:T(8,128)(2,1)S(1)}, bf16[1,128,2048]{2,1,0:T(8,128)(2,1)}, u32[]{:S(2)}) copy-start(bf16[1,128,2048]{2,1,0:T(8,128)(2,1)} %param.9) | copy-start | bytes 1572868
  0.7 37.9 %copy-start.5 = (s32[1,1024]{1,0:T(1,128)S(1)}, s32[1,1024]{1,0:T(1,128)}, u32[]{:S(2)}) copy-start(s32[1,1024]{1,0:T(1,128)} %param.6) | copy-start | bytes 12292

commit v6 on v5

--- a/solution.py
+++ b/solution.py
@@ -80,7 +80,7 @@
 
 
 def exchange_kernel(n, rows, ids_hbm, table_hbm, dy_hbm, g_hbm, xpos_ref, sums_ref, dg_ref, target_ref, over_hbm,
-                    over_ref, ids_ref, g_ref, dy_own, table, slabs, local, local_smem, x_own, x_in, dy_out, dy_in, picks, spots, dx_all, dg_parts,
+                    over_ref, ids_ref, g_ref, dy_own, table, slabs, local, local_smem, x_own, x_in, dy_out, dy_in, picks, spots, dx_all, dg_parts, dg_chips,
                     table_sem, small_sem, own_sem, x_send, x_recv, xf_send, xf_recv, dy_send, dy_recv, dyf_send, dyf_recv, dg_send, dg_recv):
     chips = n // CORES
     me = lax.axis_index('tp')
@@ -90,8 +90,8 @@
     partner = chip * CORES + 1 - core
     slots, hidden = sums_ref.shape
     barrier = pltpu.get_barrier_semaphore()
-    for step in range(1, n):
-        pl.semaphore_signal(barrier, inc=1, device_id=(dp, lax.rem(me + step, n)), device_id_type=MESH)
+    for device in [lax.rem(chip + step, chips) * CORES + core for step in range(1, chips)] + [partner]:
+        pl.semaphore_signal(barrier, inc=1, device_id=(dp, device), device_id_type=MESH)
     load_ids = pltpu.make_async_copy(ids_hbm, ids_ref, own_sem.at[0])
     load_dy = pltpu.make_async_copy(dy_hbm, dy_own, own_sem.at[1])
     load_gain = pltpu.make_async_copy(g_hbm, g_ref, own_sem.at[2])
@@ -116,7 +116,7 @@
     def device_at(step):
         return lax.rem(chip + step, chips) * CORES + core
 
-    order = list(range(2, chips - 1)) + [1, chips - 1]
+    order = list(range(2, chips - 1)) + [chips - 1, 1]
     low = me * rows
 
     load_ids.wait()
@@ -131,7 +131,7 @@
     lists = jnp.dot(hots, dy_own[...], preferred_element_type=F32).astype(BF16)
     for step in range(chips):
         dy_out[step] = lists[step * DY_ROWS:(step + 1) * DY_ROWS]
-    pl.semaphore_wait(barrier, n - 1)
+    pl.semaphore_wait(barrier, chips)
     for step in order:
         send(dy_out.at[step], dy_in.at[me], dy_send.at[step], dy_recv.at[step], device_at(step))
     send(dy_out.at[0], dy_in.at[me], dyf_send.at[0], dyf_recv.at[0], partner)
@@ -214,11 +214,14 @@
         block = source(step) * CORES + 1 - core
         remote(dy_in.at[block], dy_in.at[block], dyf_send.at[step], dyf_recv.at[step], partner).wait_recv()
         part = part + dx_of(block)
-    dg_parts[me] = part
+    dg_parts[core] = part
+    send(dg_parts.at[core], dg_parts.at[core], dg_send.at[0], dg_recv.at[0], partner)
     length = n * DY_ROWS
     sums_ref[...] = lax.dot_general(spots[...].reshape(length, slots), dx_all[...].reshape(length, hidden), TN, preferred_element_type=F32)
-    for step in range(1, n):
-        send(dg_parts.at[me], dg_parts.at[me], dg_send.at[step], dg_recv.at[step], lax.rem(me + step, n))
+    remote(dg_parts.at[1 - core], dg_parts.at[1 - core], dg_send.at[0], dg_recv.at[0], partner).wait_recv()
+    dg_chips[chip] = dg_parts[0] + dg_parts[1]
+    for step in range(1, chips):
+        send(dg_chips.at[chip], dg_chips.at[chip], dg_send.at[step], dg_recv.at[step], device_at(step))
 
     even, odd = ids_ref[pl.ds(chip * CORES, 1)], ids_ref[pl.ds(chip * CORES + 1, 1)]
     here_even, here_odd = even_first[0:1], odd_first[0:1]
@@ -242,12 +245,12 @@
         block = source(step) * CORES + core
         remote(x_in.at[block], x_in.at[block], x_send.at[step], x_recv.at[step], partner).wait_recv()
         send(x_in.at[block], x_in.at[block], xf_send.at[step], xf_recv.at[step], partner)
-    for step in range(1, n):
-        block = dg_parts.at[lax.rem(me + n - step, n)]
+    for step in range(1, chips):
+        block = dg_chips.at[source(step)]
         remote(block, block, dg_send.at[step], dg_recv.at[step], partner).wait_recv()
-    total = dg_parts[0]
-    for i in range(1, n):
-        total = total + dg_parts[i]
+    total = dg_chips[0]
+    for c in range(1, chips):
+        total = total + dg_chips[c]
     dg_ref[...] = total
     for step in [0] + order:
         block = source(step) * CORES + 1 - core
@@ -440,8 +443,8 @@
         [pltpu.SMEM((1, 1), I32), pltpu.VMEM((n, positions), I32), pltpu.VMEM((hidden // 128, 128), BF16), pltpu.VMEM((positions, hidden), BF16), pltpu.VMEM((slabs, 8, hidden), BF16), pltpu.VMEM((X_ROWS, 8, hidden), BF16), pltpu.VMEM((8, slots), I32), pltpu.SMEM((8, slots), I32),
          pltpu.VMEM((chips, X_ROWS, hidden), BF16), pltpu.VMEM((n, X_ROWS, hidden), BF16), pltpu.VMEM((chips, DY_ROWS, hidden), BF16),
          pltpu.VMEM((n, DY_ROWS, hidden), BF16), pltpu.VMEM((n, DY_ROWS, slots), BF16), pltpu.VMEM((n, DY_ROWS, slots), BF16),
-         pltpu.VMEM((n, DY_ROWS, hidden), BF16), pltpu.VMEM((n, 1, hidden), F32), dma(max(d for d in range(1, 11) if slabs % d == 0)), pltpu.SemaphoreType.DMA, dma(3)]
-        + [dma(chips)] * 8 + [dma(n)] * 2, 10**9, 48, collective_id=0, has_side_effects=True)(
+         pltpu.VMEM((n, DY_ROWS, hidden), BF16), pltpu.VMEM((CORES, 1, hidden), F32), pltpu.VMEM((chips, 1, hidden), F32), dma(max(d for d in range(1, 11) if slabs % d == 0)), pltpu.SemaphoreType.DMA, dma(3)]
+        + [dma(chips)] * 10, 10**9, 48, collective_id=0, has_side_effects=True)(
             ids, table_block.reshape(slabs, 8, hidden), grad_block.reshape(positions, hidden), gain)
     y, grad_table, dg = call(
         functools.partial(finish_kernel, zero_rows), 'finish',

time: 39.7 us -> 39.1 us (0.985)
  Pallas kernels: 37.9 us -> 37.3 us
    pallas_call x1, Pallas kernels: 26.1 us -> 25.5 us  [device_step(): call(functools.partial(exchange_kernel, n, rows), 'exchange', (shape((pos...]
where the time goes in v6:
time: 39.1 us; the launch traced here: 39 us
  Pallas kernels  37.3 us (95%)
  between operations  0.87 us (2%)
  loops' own time  0.85 us (2%)
    pallas_call x1, Pallas kernels, device_step(): call(functools.partial(exchange_kernel, n, rows), 'exchange', (shape((pos...  25.5 us
    pallas_call x1, Pallas kernels, device_step(): call(functools.partial(finish_kernel, zero_rows), 'finish', (shape((posit...  11.7 us
    another operation x1, loops' own time, device_step(): lax.while_loop(lambda carry: carry[0] > 0, general, (over[0, 0],) + result)  0.85 us

profile of v6, /device:TPU:113, one launch (start us, length us, event | category | flops | bytes accessed | tf_op | source)
XLA Modules:
  0.0 39.0 jit_solution(17871763336418968697)
XLA Ops:
  0.6 0.0 copy-start.4
  0.6 0.0 copy-start.2
  0.7 0.0 copy-start.5
  0.7 25.5 %exchange.1 = (bf16[128,2048]{1,0:T(8,128)(2,1)S(1)}, f32[160,2048]{1,0:T(8,128)S(1)}, f32[1,2048]{1,0:T(1,128)S(1)}, s32[8,160]{1,0:T(8,128)S(1)}, s32[1,1]{1,0:T(1,128)}) custom-call(s32[8,128]{1,0:T(8,128)} %bitcast.46, bf16[500,8,2048]{2,1,0:T(8,128)(2,1)} %bitcast.41, bf16[128,2048]{1,0:T(8,128)(2,1)} %bitcast.43, bf16[16,128]{1,0:T(8,128)(2,1)} %bitcast.44), custom_call_target="tpu_custom_call" | custom-call | flops 1000000000 | bytes 16777216 | tf_op jit(solution)/shard_map/exchange/pallas_call | solution.py:439
  26.2 0.0 copy-done.4
  26.2 11.7 %finish.1 = (bf16[128,2048]{1,0:T(8,128)(2,1)}, f32[4000,2048]{1,0:T(8,128)}, f32[16,128]{1,0:T(8,128)}) custom-call(s32[8,160]{1,0:T(8,128)S(1)} %get-tuple-element.55.target_ref, bf16[128,2048]{1,0:T(8,128)(2,1)S(1)} %get-tuple-element.56.xpos_ref, f32[160,2048]{1,0:T(8,128)S(1)} %get-tuple-element.57.sums_ref, bf16[16,128]{1,0:T(8,128)(2,1)S(1)} %bitcast.45, ...), custom_call_target="tpu_custom_call" | custom-call | flops 1000000000 | bytes 16777216 | tf_op jit(solution)/shard_map/finish/pallas_call | solution.py:449
  37.9 0.0 copy-done.2
  38.0 0.0 copy-done.5
  38.0 0.8 %while.13 = (s32[]{:T(128)}, bf16[1,128,2048]{2,1,0:T(8,128)(2,1)}, f32[4000,2048]{1,0:T(8,128)}, f32[2048]{0:T(1024)}, s32[8,128]{1,0:T(8,128)S(1)}, /*index=5*...) while((s32[]{:T(128)}, bf16[1,128,2048]{2,1,0:T(8,128)(2,1)}, ...), condition=%region_10.11_spmd, body=%region_0.10_spmd | while | flops 588850304 | bytes 120461624 | solution.py:461
Async XLA Ops:
  0.6 25.6 %copy-start.4 = (bf16[2048]{0:T(1024)(128)(2,1)S(1)}, bf16[2048]{0:T(1024)(128)(2,1)}, u32[]{:S(2)}) copy-start(bf16[2048]{0:T(1024)(128)(2,1)} %param.8) | copy-start | bytes 12292
  0.6 37.3 %copy-start.2 = (bf16[1,128,2048]{2,1,0:T(8,128)(2,1)S(1)}, bf16[1,128,2048]{2,1,0:T(8,128)(2,1)}, u32[]{:S(2)}) copy-start(bf16[1,128,2048]{2,1,0:T(8,128)(2,1)} %param.9) | copy-start | bytes 1572868
  0.7 37.3 %copy-start.5 = (s32[1,1024]{1,0:T(1,128)S(1)}, s32[1,1024]{1,0:T(1,128)}, u32[]{:S(2)}) copy-start(s32[1,1024]{1,0:T(1,128)} %param.6) | copy-start | bytes 12292

commit v7 on v6

--- a/solution.py
+++ b/solution.py
@@ -90,7 +90,7 @@
     partner = chip * CORES + 1 - core
     slots, hidden = sums_ref.shape
     barrier = pltpu.get_barrier_semaphore()
-    for device in [lax.rem(chip + step, chips) * CORES + core for step in range(1, chips)] + [partner]:
+    for device in [lax.rem(chip + step, chips) * CORES + core for step in list(range(2, chips - 1)) + [1, chips - 1]] + [partner]:
         pl.semaphore_signal(barrier, inc=1, device_id=(dp, device), device_id_type=MESH)
     load_ids = pltpu.make_async_copy(ids_hbm, ids_ref, own_sem.at[0])
     load_dy = pltpu.make_async_copy(dy_hbm, dy_own, own_sem.at[1])
@@ -264,6 +264,8 @@
 def finish_kernel(zero_rows, target_ref, xpos_ref, sums_ref, g_ref, dg_in, y_hbm, de_ref, dg_hbm, zeros, targets, y_ref, dg_ref, zero_sem, row_sem, small_sem, out_sem):
     blocks = de_ref.shape[0] // zero_rows
     slots = sums_ref.shape[0]
+    to_smem = pltpu.make_async_copy(target_ref, targets, small_sem)
+    to_smem.start()
     zeros[...] = jnp.zeros_like(zeros)
 
     def zero_copy(i):
@@ -271,8 +273,6 @@
 
     for i in range(blocks):
         zero_copy(i).start()
-    to_smem = pltpu.make_async_copy(target_ref, targets, small_sem)
-    to_smem.start()
     gain = wide(g_ref[...]).astype(BF16)
     h = xpos_ref[...].astype(F32)
     y_ref[...] = (h * rms(h)).astype(BF16) * gain

time: 39.1 us -> 39.1 us (level)
  no operation moved by 1% of the time
where the time goes in v7:
time: 39.1 us; the launch traced here: 39 us
  Pallas kernels  37.3 us (95%)
  between operations  0.87 us (2%)
  loops' own time  0.85 us (2%)
    pallas_call x1, Pallas kernels, device_step(): call(functools.partial(exchange_kernel, n, rows), 'exchange', (shape((pos...  25.5 us
    pallas_call x1, Pallas kernels, device_step(): call(functools.partial(finish_kernel, zero_rows), 'finish', (shape((posit...  11.7 us
    another operation x1, loops' own time, device_step(): lax.while_loop(lambda carry: carry[0] > 0, general, (over[0, 0],) + result)  0.85 us

profile of v7, /device:TPU:113, one launch (start us, length us, event | category | flops | bytes accessed | tf_op | source)
XLA Modules:
  0.0 39.0 jit_solution(4492143328235861859)
XLA Ops:
  0.6 0.0 copy-start.4
  0.6 0.0 copy-start.2
  0.7 0.0 copy-start.5
  0.7 25.5 %exchange.1 = (bf16[128,2048]{1,0:T(8,128)(2,1)S(1)}, f32[160,2048]{1,0:T(8,128)S(1)}, f32[1,2048]{1,0:T(1,128)S(1)}, s32[8,160]{1,0:T(8,128)S(1)}, s32[1,1]{1,0:T(1,128)}) custom-call(s32[8,128]{1,0:T(8,128)} %bitcast.46, bf16[500,8,2048]{2,1,0:T(8,128)(2,1)} %bitcast.41, bf16[128,2048]{1,0:T(8,128)(2,1)} %bitcast.43, bf16[16,128]{1,0:T(8,128)(2,1)} %bitcast.44), custom_call_target="tpu_custom_call" | custom-call | flops 1000000000 | bytes 16777216 | tf_op jit(solution)/shard_map/exchange/pallas_call | solution.py:439
  26.2 0.0 copy-done.4
  26.2 11.7 %finish.1 = (bf16[128,2048]{1,0:T(8,128)(2,1)}, f32[4000,2048]{1,0:T(8,128)}, f32[16,128]{1,0:T(8,128)}) custom-call(s32[8,160]{1,0:T(8,128)S(1)} %get-tuple-element.55.target_ref, bf16[128,2048]{1,0:T(8,128)(2,1)S(1)} %get-tuple-element.56.xpos_ref, f32[160,2048]{1,0:T(8,128)S(1)} %get-tuple-element.57.sums_ref, bf16[16,128]{1,0:T(8,128)(2,1)S(1)} %bitcast.45, ...), custom_call_target="tpu_custom_call" | custom-call | flops 1000000000 | bytes 16777216 | tf_op jit(solution)/shard_map/finish/pallas_call | solution.py:449
  37.9 0.0 copy-done.2
  38.0 0.0 copy-done.5
  38.0 0.8 %while.13 = (s32[]{:T(128)}, bf16[1,128,2048]{2,1,0:T(8,128)(2,1)}, f32[4000,2048]{1,0:T(8,128)}, f32[2048]{0:T(1024)}, s32[8,128]{1,0:T(8,128)S(1)}, /*index=5*...) while((s32[]{:T(128)}, bf16[1,128,2048]{2,1,0:T(8,128)(2,1)}, ...), condition=%region_10.11_spmd, body=%region_0.10_spmd | while | flops 588850304 | bytes 120461624 | solution.py:461
Async XLA Ops:
  0.6 25.6 %copy-start.4 = (bf16[2048]{0:T(1024)(128)(2,1)S(1)}, bf16[2048]{0:T(1024)(128)(2,1)}, u32[]{:S(2)}) copy-start(bf16[2048]{0:T(1024)(128)(2,1)} %param.8) | copy-start | bytes 12292
  0.6 37.3 %copy-start.2 = (bf16[1,128,2048]{2,1,0:T(8,128)(2,1)S(1)}, bf16[1,128,2048]{2,1,0:T(8,128)(2,1)}, u32[]{:S(2)}) copy-start(bf16[1,128,2048]{2,1,0:T(8,128)(2,1)} %param.9) | copy-start | bytes 1572868
  0.7 37.3 %copy-start.5 = (s32[1,1024]{1,0:T(1,128)S(1)}, s32[1,1024]{1,0:T(1,128)}, u32[]{:S(2)}) copy-start(s32[1,1024]{1,0:T(1,128)} %param.6) | copy-start | bytes 12292
